TPU v7x, 128 devices: a whole 4x4x4 slice. The times are simulated.
128 devices in a mesh: rep: 2 (over core), rows: 64 (over z, y, x).
Axes of the slice: x: 4, y: 4, z: 4, core: 2. Of those that a mesh axis runs over, the one named last changes fastest.
Arguments:
- adjacency: bfloat16 [24576, 24576], P('rows', 'rep')
- block_mask: int32 [64, 64], replicated
- features: bfloat16 [24576, 200], P('rows')
- w_one: bfloat16 [200, 512], replicated
- w_two: bfloat16 [512, 107], replicated
Outputs:
- output: float32 [24576, 107], P('rows')
All inputs are finite; a program needn't handle non-finite values.
Results may differ from a plain program's by a relative error of at most 0.001.
Values are sent between devices in bfloat16 or wider.
A program may use at most 1 GiB of HBM per device.

v0:
```python
import jax
import jax.numpy as jnp
from jax import lax
from jax.sharding import PartitionSpec as P


def solution(mesh):
    rep_size = mesh.shape['rep']
    rows_size = mesh.shape['rows']
    stage_count = rows_size // rep_size
    perm_pairs = [(src_rep * rows_size + src_row, (src_row // stage_count) * rows_size + (src_row % stage_count) * rep_size + src_rep) for src_rep in range(rep_size) for src_row in range(rows_size)]

    def range_rows(feat_blk):
        rep_idx = lax.axis_index('rep')
        piece_rows = feat_blk.shape[0] // rep_size
        send_piece = lax.dynamic_slice_in_dim(feat_blk, rep_idx * piece_rows, piece_rows, 0)
        recv_piece = lax.ppermute(send_piece, ('rep', 'rows'), perm_pairs)
        return lax.all_gather(recv_piece, 'rows', axis=0, tiled=True)

    def aggregate(adj_local, block_mask, feat_blk):
        rows_idx = lax.axis_index('rows')
        rep_idx = lax.axis_index('rep')
        gathered = range_rows(feat_blk)
        blk_rows = feat_blk.shape[0]
        feat_width = feat_blk.shape[1]
        mask_part = lax.dynamic_slice(block_mask, (rows_idx, rep_idx * stage_count), (1, stage_count))
        masked = (gathered.reshape(stage_count, blk_rows, feat_width) * mask_part.astype(gathered.dtype).reshape(stage_count, 1, 1)).reshape(stage_count * blk_rows, feat_width)
        part_sum = jnp.dot(adj_local, masked, preferred_element_type=jnp.float32)
        return lax.psum(part_sum, 'rep').astype(jnp.bfloat16)

    def local_fn(adj_local, block_mask, feat_blk, w_one, w_two):
        y_one = aggregate(adj_local, block_mask, feat_blk)
        z_one = jnp.maximum(jnp.dot(y_one, w_one, preferred_element_type=jnp.float32), 0.0).astype(jnp.bfloat16)
        y_two = aggregate(adj_local, block_mask, z_one)
        return jnp.dot(y_two, w_two, preferred_element_type=jnp.float32)

    return jax.shard_map(local_fn, mesh=mesh, in_specs=(P('rows', 'rep'), P(), P('rows', None), P(), P()), out_specs=P('rows', None), check_vma=False)
```

profile of v0, /device:TPU:1, one launch (start us, length us, event | category | flops | bytes accessed | tf_op | source)
XLA Modules:
  0.0 239.3 jit_solution(1414347635702480177)
XLA Ops:
  6.5 0.0 copy-start
  6.5 0.0 all-gather.3.cloned.1.call-start
  6.5 1.0 constant_dynamic-slice_fusion
  7.6 0.1 copy.7
  7.7 4.5 %collective-permute-start = (bf16[192,200]{1,0:T(8,128)(2,1)S(1)}, bf16[192,200]{1,0:T(8,128)(2,1)S(1)}, u32[]{:S(2)}, u32[]{:S(2)}) collective-permute-start(bf16[192,200]{1,0:T(8,128)(2,1)S(1)} %copy.7), channel_id=1, source_target_pairs={{0,0},{1,2},{2,4},{3,6},{4,8},{5,10},{6,12},{7,14},{8,16},{9,18},{... | collective-permute-start | bytes 230408 | tf_op jit(solution)/shard_map/ppermute | solution.py:17
  12.2 4.7 %collective-permute-done = bf16[192,200]{1,0:T(8,128)(2,1)S(1)} collective-permute-done((bf16[192,200]{1,0:T(8,128)(2,1)S(1)}, bf16[192,200]{1,0:T(8,128)(2,1)S(1)}, u32[]{:S(2)}, u32[]{:S(2)}) %collective-permute-start) | collective-permute-done | bytes 76832 | tf_op jit(solution)/shard_map/ppermute | solution.py:17
  16.9 0.6 copy-done.3
  17.5 0.0 all-gather.3.cloned.1.call-update
  17.6 0.0 all-gather.5.cloned.1.call-start
  17.6 0.8 convert_bitcast_fusion
  18.4 0.1 mul.35
  18.5 74.7 %all-gather.3.cloned.1.call-done = bf16[12288,200]{1,0:T(8,128)(2,1)} async-done(((bf16[192,200]{1,0:T(8,128)(2,1)}), bf16[12288,200]{1,0:T(8,128)(2,1)}) %all-gather.3.cloned.1.call-update) | async-done | bytes 4915216 | tf_op jit(solution)/shard_map/all_gather | solution.py:18
  93.2 8.7 %fusion.9 = f32[384,200]{0,1:T(8,128)S(1)} fusion(bf16[384,12288]{1,0:T(8,128)(2,1)} %param.5, bf16[12288,200]{1,0:T(8,128)(2,1)} %all-gather.3.cloned.1.call-done, bf16[12288]{0:T(1024)(128)(2,1)S(1)} %mul.36), kind=kOutput, calls=%fused_computation.7 | convolution fusion | flops 1889894400 | bytes 14684160 | tf_op jit(solution)/shard_map/dot_general | solution.py:28
  102.0 5.3 %all-reduce.2 = bf16[384,200]{0,1:T(8,128)(2,1)S(1)} all-reduce(f32[384,200]{0,1:T(8,128)S(1)} %fusion.9), channel_id=1, replica_groups=mesh['rep'=2,'rows'=64] {'rep'}, use_global_device_ids=true, to_apply=%region_0.0 | all-reduce | flops 76800 | bytes 460800 | tf_op jit(solution)/shard_map/psum | solution.py:29
  107.3 0.3 fusion.18
  107.6 3.2 %collective-permute-start.1 = (bf16[192,512]{1,0:T(8,128)(2,1)S(1)}, bf16[192,512]{1,0:T(8,128)(2,1)S(1)}, u32[]{:S(2)}, u32[]{:S(2)}) collective-permute-start(bf16[192,512]{1,0:T(8,128)(2,1)S(1)} %fusion.12), channel_id=1, source_target_pairs={{0,0},{1,2},{2,4},{3,6},{4,8},{5,10},{6,12},{7,14},{8,16},{9,18},{... | collective-permute-start | bytes 589832 | tf_op jit(solution)/shard_map/ppermute | solution.py:17
  110.9 5.2 %collective-permute-done.1 = bf16[192,512]{1,0:T(8,128)(2,1)S(1)} collective-permute-done((bf16[192,512]{1,0:T(8,128)(2,1)S(1)}, bf16[192,512]{1,0:T(8,128)(2,1)S(1)}, u32[]{:S(2)}, u32[]{:S(2)}) %collective-permute-start.1) | collective-permute-done | bytes 196640 | tf_op jit(solution)/shard_map/ppermute | solution.py:17
  116.1 0.7 copy-done.1
  116.8 0.0 all-gather.5.cloned.1.call-update
  116.8 0.0 copy-start.2
  116.8 92.7 %all-gather.5.cloned.1.call-done = bf16[12288,512]{1,0:T(8,128)(2,1)} async-done(((bf16[192,512]{1,0:T(8,128)(2,1)}), bf16[12288,512]{1,0:T(8,128)(2,1)}) %all-gather.5.cloned.1.call-update) | async-done | bytes 12582928 | tf_op jit(solution)/shard_map/all_gather | solution.py:18
  209.5 15.7 %fusion.6 = f32[384,512]{0,1:T(8,128)S(1)} fusion(bf16[384,12288]{1,0:T(8,128)(2,1)} %param.5, bf16[12288,512]{1,0:T(8,128)(2,1)} %all-gather.5.cloned.1.call-done, bf16[12288]{0:T(1024)(128)(2,1)S(1)} %mul.36), kind=kOutput, calls=%fused_computation.6 | convolution fusion | flops 4838129664 | bytes 22831104 | tf_op jit(solution)/shard_map/dot_general | solution.py:28
  225.2 6.3 %all-reduce.3 = bf16[384,512]{0,1:T(8,128)(2,1)S(1)} all-reduce(f32[384,512]{0,1:T(8,128)S(1)} %fusion.6), channel_id=1, replica_groups=mesh['rep'=2,'rows'=64] {'rep'}, use_global_device_ids=true, to_apply=%region_1.0 | all-reduce | flops 196608 | bytes 1179648 | tf_op jit(solution)/shard_map/psum | solution.py:29
  231.6 0.9 fusion.17
  (6 shorter events, 0.1 us)
Async XLA Ops:
  6.5 100.7 %copy-start = (bf16[200,512]{1,0:T(8,128)(2,1)S(1)}, bf16[200,512]{1,0:T(8,128)(2,1)}, u32[]{:S(2)}) copy-start(bf16[200,512]{1,0:T(8,128)(2,1)} %param.8) | copy-start | bytes 614404
  6.5 86.7 %all-gather.3.cloned.1.call-start = ((), (), s32[]{:S(2)}) async-start(), calls=%async_computation | async-start | bytes 6389760 | tf_op jit(solution)/shard_map/all_gather | solution.py:18
  7.7 9.2 %collective-permute-start = (bf16[192,200]{1,0:T(8,128)(2,1)S(1)}, bf16[192,200]{1,0:T(8,128)(2,1)S(1)}, u32[]{:S(2)}, u32[]{:S(2)}) collective-permute-start(bf16[192,200]{1,0:T(8,128)(2,1)S(1)} %copy.7), channel_id=1, source_target_pairs={{0,0},{1,2},{2,4},{3,6},{4,8},{5,10},{6,12},{7,14},{8,16},{9,18},{... | collective-permute-start | bytes 230408 | tf_op jit(solution)/shard_map/ppermute | solution.py:17
  16.9 0.6 copy-start.3
  17.6 192.0 %all-gather.5.cloned.1.call-start = ((), (), s32[]{:S(2)}) async-start(), calls=%async_computation.1 | async-start | bytes 12779520 | tf_op jit(solution)/shard_map/all_gather | solution.py:18
  107.6 8.5 %collective-permute-start.1 = (bf16[192,512]{1,0:T(8,128)(2,1)S(1)}, bf16[192,512]{1,0:T(8,128)(2,1)S(1)}, u32[]{:S(2)}, u32[]{:S(2)}) collective-permute-start(bf16[192,512]{1,0:T(8,128)(2,1)S(1)} %fusion.12), channel_id=1, source_target_pairs={{0,0},{1,2},{2,4},{3,6},{4,8},{5,10},{6,12},{7,14},{8,16},{9,18},{... | collective-permute-start | bytes 589832 | tf_op jit(solution)/shard_map/ppermute | solution.py:17
  116.1 0.7 copy-start.1
  116.8 114.7 %copy-start.2 = (bf16[512,107]{0,1:T(8,128)(2,1)S(1)}, bf16[512,107]{0,1:T(8,128)(2,1)}, u32[]{:S(2)}) copy-start(bf16[512,107]{0,1:T(8,128)(2,1)} %param.9) | copy-start | bytes 328708
Sparse Core Ops, SparseCore 0:
  17.7 75.5 all-gather.2
  116.9 92.5 all-gather.4
where the time goes:
time: 239 us
  waiting for transfers between devices  177 us (74%)
  matrix products  25.6 us (11%)
  between operations  13.5 us (6%)
  blocking collectives  11.6 us (5%)
  starting transfers between devices  7.81 us (3%)
  local copies, waits for them, and re-layouts  2.55 us (1%)
    all_gather x2, waiting for transfers between devices, range_rows(): return lax.all_gather(recv_piece, 'rows', axis=0, tiled=True)  167 us
    dot_general x2, matrix products, aggregate(): part_sum = jnp.dot(adj_local, masked, preferred_element_type=jnp.float32)  24.4 us
    psum x2, blocking collectives, aggregate(): return lax.psum(part_sum, 'rep').astype(jnp.bfloat16)  11.6 us
    ppermute x2, waiting for transfers between devices, range_rows(): recv_piece = lax.ppermute(send_piece, ('rep', 'rows'), perm_pairs)  9.91 us
    ppermute x2, starting transfers between devices, range_rows(): recv_piece = lax.ppermute(send_piece, ('rep', 'rows'), perm_pairs)  7.77 us
  transfers between devices with their start and end apart: 4, of which 4 were waited for; matrix products, arithmetic and copies ran while one was open for 0% of the time, Pallas kernels for 0%

commit v1 on v0

--- a/solution.py
+++ b/solution.py
@@ -17,19 +17,18 @@
         recv_piece = lax.ppermute(send_piece, ('rep', 'rows'), perm_pairs)
         return lax.all_gather(recv_piece, 'rows', axis=0, tiled=True)
 
-    def aggregate(adj_local, block_mask, feat_blk):
+    def aggregate(adj_local, block_mask, gathered):
         rows_idx = lax.axis_index('rows')
         rep_idx = lax.axis_index('rep')
-        gathered = range_rows(feat_blk)
-        blk_rows = feat_blk.shape[0]
-        feat_width = feat_blk.shape[1]
+        blk_rows = adj_local.shape[0]
+        feat_width = gathered.shape[1]
         mask_part = lax.dynamic_slice(block_mask, (rows_idx, rep_idx * stage_count), (1, stage_count))
         masked = (gathered.reshape(stage_count, blk_rows, feat_width) * mask_part.astype(gathered.dtype).reshape(stage_count, 1, 1)).reshape(stage_count * blk_rows, feat_width)
         part_sum = jnp.dot(adj_local, masked, preferred_element_type=jnp.float32)
         return lax.psum(part_sum, 'rep').astype(jnp.bfloat16)
 
     def local_fn(adj_local, block_mask, feat_blk, w_one, w_two):
-        y_one = aggregate(adj_local, block_mask, feat_blk)
+        y_one = range_rows(aggregate(adj_local, block_mask, range_rows(feat_blk)))
         z_one = jnp.maximum(jnp.dot(y_one, w_one, preferred_element_type=jnp.float32), 0.0).astype(jnp.bfloat16)
         y_two = aggregate(adj_local, block_mask, z_one)
         return jnp.dot(y_two, w_two, preferred_element_type=jnp.float32)

time: 239 us -> 215 us (0.90)
  waiting for transfers between devices: 177 us -> 157 us
  matrix products: 25.6 us -> 20.9 us
    all_gather x2, waiting for transfers between devices: 167 us -> 148 us  [range_rows(): return lax.all_gather(recv_piece, 'rows', axis=0, tiled=True)]
    dot_general x2, matrix products: 24.4 us -> 20 us  [aggregate(): part_sum = jnp.dot(adj_local, masked, preferred_element_type=jnp.float32)]
where the time goes in v1:
time: 215 us
  waiting for transfers between devices  157 us (73%)
  matrix products  20.9 us (10%)
  between operations  13.5 us (6%)
  blocking collectives  12.1 us (6%)
  starting transfers between devices  7.62 us (4%)
  local copies, waits for them, and re-layouts  2.53 us (1%)
    all_gather x2, waiting for transfers between devices, range_rows(): return lax.all_gather(recv_piece, 'rows', axis=0, tiled=True)  148 us
    dot_general x2, matrix products, aggregate(): part_sum = jnp.dot(adj_local, masked, preferred_element_type=jnp.float32)  20 us
    psum x2, blocking collectives, aggregate(): return lax.psum(part_sum, 'rep').astype(jnp.bfloat16)  12.1 us
    ppermute x2, waiting for transfers between devices, range_rows(): recv_piece = lax.ppermute(send_piece, ('rep', 'rows'), perm_pairs)  9.05 us
    ppermute x2, starting transfers between devices, range_rows(): recv_piece = lax.ppermute(send_piece, ('rep', 'rows'), perm_pairs)  7.58 us
  transfers between devices with their start and end apart: 4, of which 4 were waited for; matrix products, arithmetic and copies ran while one was open for 0% of the time, Pallas kernels for 0%

profile of v1, /device:TPU:1, one launch (start us, length us, event | category | flops | bytes accessed | tf_op | source)
XLA Modules:
  0.0 214.5 jit_solution(12250129012132498981)
XLA Ops:
  6.5 0.0 copy-start
  6.5 0.0 all-gather.3.cloned.1.call-start
  6.5 1.0 constant_dynamic-slice_fusion
  7.6 0.1 copy.7
  7.7 4.5 %collective-permute-start = (bf16[192,200]{1,0:T(8,128)(2,1)S(1)}, bf16[192,200]{1,0:T(8,128)(2,1)S(1)}, u32[]{:S(2)}, u32[]{:S(2)}) collective-permute-start(bf16[192,200]{1,0:T(8,128)(2,1)S(1)} %copy.7), channel_id=1, source_target_pairs={{0,0},{1,2},{2,4},{3,6},{4,8},{5,10},{6,12},{7,14},{8,16},{9,18},{... | collective-permute-start | bytes 230408 | tf_op jit(solution)/shard_map/ppermute | solution.py:17
  12.2 4.7 %collective-permute-done = bf16[192,200]{1,0:T(8,128)(2,1)S(1)} collective-permute-done((bf16[192,200]{1,0:T(8,128)(2,1)S(1)}, bf16[192,200]{1,0:T(8,128)(2,1)S(1)}, u32[]{:S(2)}, u32[]{:S(2)}) %collective-permute-start) | collective-permute-done | bytes 76832 | tf_op jit(solution)/shard_map/ppermute | solution.py:17
  16.9 0.6 copy-done.2
  17.5 0.0 all-gather.3.cloned.1.call-update
  17.6 0.0 all-gather.5.cloned.1.call-start
  17.6 0.8 convert_bitcast_fusion
  18.4 0.1 mul.35
  18.5 74.7 %all-gather.3.cloned.1.call-done = bf16[12288,200]{1,0:T(8,128)(2,1)} async-done(((bf16[192,200]{1,0:T(8,128)(2,1)}), bf16[12288,200]{1,0:T(8,128)(2,1)}) %all-gather.3.cloned.1.call-update) | async-done | bytes 4915216 | tf_op jit(solution)/shard_map/all_gather | solution.py:18
  93.2 7.1 %fusion.6 = f32[384,200]{1,0:T(8,128)S(1)} fusion(bf16[384,12288]{1,0:T(8,128)(2,1)} %param.5, bf16[12288,200]{1,0:T(8,128)(2,1)} %all-gather.3.cloned.1.call-done, bf16[12288]{0:T(1024)(128)(2,1)S(1)} %mul.36), kind=kOutput, calls=%fused_computation.7 | convolution fusion | flops 1889894400 | bytes 14684160 | tf_op jit(solution)/shard_map/dot_general | solution.py:27
  100.3 5.6 %all-reduce.2 = bf16[384,200]{1,0:T(8,128)(2,1)S(1)} all-reduce(f32[384,200]{1,0:T(8,128)S(1)} %fusion.6), channel_id=1, replica_groups=mesh['rep'=2,'rows'=64] {'rep'}, use_global_device_ids=true, to_apply=%region_0.0 | all-reduce | flops 76800 | bytes 460800 | tf_op jit(solution)/shard_map/psum | solution.py:28
  105.9 3.1 %collective-permute-start.1 = (bf16[192,200]{1,0:T(8,128)(2,1)S(1)}, bf16[192,200]{1,0:T(8,128)(2,1)S(1)}, u32[]{:S(2)}, u32[]{:S(2)}) collective-permute-start(bf16[192,200]{1,0:T(8,128)(2,1)S(1)} %dynamic-slice_convert_fusion), channel_id=1, source_target_pairs={{0,0},{1,2},{2,4},{3,6},{4,8},{5,10},{6,12},{7,14},{8,16},{9,18},{... | collective-permute-start | bytes 230408 | tf_op jit(solution)/shard_map/ppermute | solution.py:17
  108.9 4.4 %collective-permute-done.1 = bf16[192,200]{1,0:T(8,128)(2,1)S(1)} collective-permute-done((bf16[192,200]{1,0:T(8,128)(2,1)S(1)}, bf16[192,200]{1,0:T(8,128)(2,1)S(1)}, u32[]{:S(2)}, u32[]{:S(2)}) %collective-permute-start.1) | collective-permute-done | bytes 76832 | tf_op jit(solution)/shard_map/ppermute | solution.py:17
  113.3 0.6 copy-done.3
  114.0 0.0 all-gather.5.cloned.1.call-update
  114.0 0.0 copy-start.1
  114.0 73.3 %all-gather.5.cloned.1.call-done = bf16[12288,200]{1,0:T(8,128)(2,1)} async-done(((bf16[192,200]{1,0:T(8,128)(2,1)}), bf16[12288,200]{1,0:T(8,128)(2,1)}) %all-gather.5.cloned.1.call-update) | async-done | bytes 4915216 | tf_op jit(solution)/shard_map/all_gather | solution.py:18
  187.3 0.0 copy-done
  187.3 13.0 %fusion.5 = f32[384,512]{0,1:T(8,128)S(1)} fusion(bf16[384,12288]{1,0:T(8,128)(2,1)} %param.5, bf16[12288,200]{1,0:T(8,128)(2,1)} %all-gather.5.cloned.1.call-done, bf16[200,512]{1,0:T(8,128)(2,1)S(1)} %copy-done, bf16[12288]{0:T(1024)(128)(2,1)S(1)} %mul.36), kind=kOutput, calls=%fused_computation.6 | convolution fusion | flops 7367294976 | bytes 15368192 | tf_op jit(solution)/shard_map/dot_general | solution.py:27
  200.2 6.6 %all-reduce.3 = bf16[384,512]{0,1:T(8,128)(2,1)S(1)} all-reduce(f32[384,512]{0,1:T(8,128)S(1)} %fusion.5), channel_id=1, replica_groups=mesh['rep'=2,'rows'=64] {'rep'}, use_global_device_ids=true, to_apply=%region_1.0 | all-reduce | flops 196608 | bytes 1179648 | tf_op jit(solution)/shard_map/psum | solution.py:28
  206.8 0.9 fusion.12
  (5 shorter events, 0.0 us)
Async XLA Ops:
  6.5 180.7 %copy-start = (bf16[200,512]{1,0:T(8,128)(2,1)S(1)}, bf16[200,512]{1,0:T(8,128)(2,1)}, u32[]{:S(2)}) copy-start(bf16[200,512]{1,0:T(8,128)(2,1)} %param.8) | copy-start | bytes 614404
  6.5 86.7 %all-gather.3.cloned.1.call-start = ((), (), s32[]{:S(2)}) async-start(), calls=%async_computation | async-start | bytes 6389760 | tf_op jit(solution)/shard_map/all_gather | solution.py:18
  7.7 9.2 %collective-permute-start = (bf16[192,200]{1,0:T(8,128)(2,1)S(1)}, bf16[192,200]{1,0:T(8,128)(2,1)S(1)}, u32[]{:S(2)}, u32[]{:S(2)}) collective-permute-start(bf16[192,200]{1,0:T(8,128)(2,1)S(1)} %copy.7), channel_id=1, source_target_pairs={{0,0},{1,2},{2,4},{3,6},{4,8},{5,10},{6,12},{7,14},{8,16},{9,18},{... | collective-permute-start | bytes 230408 | tf_op jit(solution)/shard_map/ppermute | solution.py:17
  16.9 0.6 copy-start.2
  17.6 169.7 %all-gather.5.cloned.1.call-start = ((), (), s32[]{:S(2)}) async-start(), calls=%async_computation.1 | async-start | bytes 6389760 | tf_op jit(solution)/shard_map/all_gather | solution.py:18
  105.9 7.4 %collective-permute-start.1 = (bf16[192,200]{1,0:T(8,128)(2,1)S(1)}, bf16[192,200]{1,0:T(8,128)(2,1)S(1)}, u32[]{:S(2)}, u32[]{:S(2)}) collective-permute-start(bf16[192,200]{1,0:T(8,128)(2,1)S(1)} %dynamic-slice_convert_fusion), channel_id=1, source_target_pairs={{0,0},{1,2},{2,4},{3,6},{4,8},{5,10},{6,12},{7,14},{8,16},{9,18},{... | collective-permute-start | bytes 230408 | tf_op jit(solution)/shard_map/ppermute | solution.py:17
  113.3 0.6 copy-start.3
  114.0 92.8 %copy-start.1 = (bf16[512,107]{0,1:T(8,128)(2,1)S(1)}, bf16[512,107]{0,1:T(8,128)(2,1)}, u32[]{:S(2)}) copy-start(bf16[512,107]{0,1:T(8,128)(2,1)} %param.9) | copy-start | bytes 328708
Sparse Core Ops, SparseCore 0:
  17.7 75.5 all-gather.2
  114.1 73.1 all-gather.4

commit v2 on v1

v2 whole, which is shorter than its diff:
```python
import jax
import jax.numpy as jnp
from jax import lax
from jax.experimental import pallas as pl
from jax.experimental.pallas import tpu as pltpu
from jax.sharding import PartitionSpec as P

BLOCK = 384
F0, F1, F2 = 200, 512, 107
PART = 128
SLOTS = 96
CHUNK = 4
AXES = ('xyz', 'yzx', 'zxy')
MESH = pl.DeviceIdType.MESH

SRC_ORDER = [
    (0, 0, 0, 0), (1, 0, 0, 0), (2, 0, 0, 0), (0, 0, 0, 1), (0, 0, 0, 3), (0, 0, 1, 0), (0, 0, 3, 0), (0, 1, 0, 0), (1, 0, 0, 1), (1, 0, 0, 3), (1, 0, 1, 0), (1, 0, 3, 0),
    (1, 1, 0, 0), (2, 0, 0, 1), (2, 0, 0, 3), (2, 0, 1, 0), (2, 0, 3, 0), (2, 1, 0, 0), (0, 0, 1, 1), (0, 0, 3, 1), (0, 1, 0, 1), (0, 0, 0, 2), (0, 0, 1, 3), (0, 0, 3, 3),
    (0, 1, 0, 3), (1, 0, 1, 1), (1, 0, 0, 2), (0, 0, 2, 0), (0, 1, 1, 0), (1, 0, 3, 1), (2, 0, 1, 1), (1, 0, 1, 3), (0, 1, 3, 0), (1, 0, 2, 0), (2, 0, 1, 3), (1, 0, 3, 3),
    (1, 1, 0, 1), (1, 1, 1, 0), (2, 0, 3, 1), (1, 1, 3, 0), (2, 1, 1, 0), (1, 1, 0, 3), (2, 0, 3, 3), (0, 0, 2, 1), (2, 1, 0, 1), (0, 1, 1, 1), (2, 0, 0, 2), (0, 0, 1, 2),
    (1, 0, 1, 2), (2, 0, 2, 0), (0, 1, 3, 1), (0, 0, 2, 3), (1, 0, 3, 2), (2, 1, 3, 0), (2, 1, 0, 3), (0, 0, 3, 2), (0, 1, 0, 2), (1, 0, 2, 1), (2, 0, 2, 1), (1, 0, 2, 3),
    (1, 1, 0, 2), (2, 0, 2, 3), (0, 1, 1, 3), (1, 1, 1, 3), (1, 1, 1, 1), (2, 1, 2, 0), (0, 1, 3, 3), (1, 1, 3, 1), (2, 1, 3, 1), (1, 1, 3, 3), (0, 1, 2, 0), (2, 0, 3, 2),
    (2, 1, 1, 1), (2, 0, 1, 2), (2, 1, 0, 2), (1, 1, 2, 0), (2, 1, 3, 3), (0, 0, 2, 2), (2, 1, 1, 3), (2, 1, 2, 1), (1, 0, 2, 2), (0, 1, 2, 1), (2, 0, 2, 2), (1, 1, 1, 2),
    (1, 1, 2, 1), (0, 1, 1, 2), (2, 1, 2, 3), (1, 1, 3, 2), (0, 1, 2, 3), (1, 1, 2, 3), (0, 1, 3, 2), (2, 1, 1, 2), (2, 1, 3, 2), (0, 1, 2, 2), (1, 1, 2, 2), (2, 1, 2, 2),
]
SINK_ORDER = [
    (0, 0, 0, 0), (1, 0, 0, 0), (2, 0, 0, 0), (0, 0, 0, 1), (0, 0, 0, 3), (0, 0, 1, 0), (1, 0, 0, 1), (1, 0, 0, 3), (0, 0, 3, 0), (2, 0, 1, 0), (0, 1, 0, 0), (1, 0, 1, 0),
    (2, 0, 0, 1), (2, 0, 3, 0), (1, 0, 3, 0), (2, 0, 0, 3), (0, 1, 0, 1), (1, 1, 0, 0), (2, 1, 0, 0), (0, 0, 1, 1), (0, 0, 3, 1), (2, 0, 3, 1), (1, 0, 0, 2), (0, 0, 0, 2),
    (0, 1, 0, 3), (2, 0, 2, 0), (0, 0, 1, 3), (2, 0, 1, 1), (1, 0, 1, 1), (1, 0, 1, 3), (0, 0, 3, 3), (2, 0, 3, 3), (0, 1, 1, 0), (0, 0, 2, 0), (1, 0, 3, 1), (2, 0, 1, 3),
    (1, 0, 3, 3), (1, 0, 2, 0), (2, 1, 3, 0), (2, 0, 0, 2), (0, 1, 3, 0), (0, 0, 2, 1), (1, 1, 0, 1), (2, 1, 1, 0), (1, 1, 0, 3), (0, 1, 1, 1), (1, 1, 1, 0), (2, 1, 0, 1),
    (2, 1, 0, 3), (0, 0, 1, 2), (1, 0, 1, 2), (1, 1, 3, 0), (2, 0, 2, 1), (0, 1, 3, 1), (2, 0, 2, 3), (1, 0, 3, 2), (0, 0, 2, 3), (2, 1, 2, 0), (0, 0, 3, 2), (2, 0, 1, 2),
    (2, 0, 3, 2), (1, 0, 2, 1), (0, 1, 0, 2), (1, 1, 0, 2), (1, 0, 2, 3), (0, 1, 1, 3), (2, 1, 1, 1), (2, 1, 3, 1), (2, 1, 0, 2), (0, 1, 1, 2), (0, 1, 3, 3), (0, 1, 2, 0),
    (1, 1, 1, 1), (1, 1, 1, 3), (1, 1, 2, 0), (0, 1, 2, 1), (2, 1, 1, 3), (2, 1, 3, 3), (1, 1, 3, 1), (1, 1, 3, 3), (0, 0, 2, 2), (0, 1, 2, 3), (2, 0, 2, 2), (1, 0, 2, 2),
    (0, 1, 2, 2), (0, 1, 3, 2), (1, 1, 1, 2), (2, 1, 2, 3), (1, 1, 3, 2), (1, 1, 2, 1), (2, 1, 1, 2), (2, 1, 2, 1), (1, 1, 2, 3), (2, 1, 3, 2), (1, 1, 2, 2), (2, 1, 2, 2),
]


def relay_bit(p, axis, off):
    before = AXES[p][:AXES[p].index(axis)]
    return sum(off[a] for a in before) % 2


def piece_sends(is_src, p, zc, dy, dx):
    off = {'x': dx, 'y': dy, 'z': zc}
    order = AXES[p]
    last = -1
    for i, a in enumerate(order):
        if (off[a] != 0) if a != 'z' else (not is_src or zc == 1):
            last = i
    out = []
    if last >= 0:
        a = order[last]
        bit = relay_bit(p, a, off)
        if a in 'xy':
            if off[a] == 3 and bit == 0:
                out.append((a, 1))
            if off[a] == 1 and bit == 1:
                out.append((a, -1))
        elif is_src and zc == 1 and bit == 0:
            out.append(('z', -1))
        elif not is_src and zc == 0 and bit == 1:
            out.append(('z', -1))
    for a in order[last + 1:]:
        out += [(a, 1), (a, -1)]
    return out


def kernel(adj, mask, h0, w1, w2, out, a_v, h0_v, w1_v, w1t, w2_v, tab1, tab2, acc1, acc2, peer1, peer2,
           load_sem, recv_sem1, recv_sem2, send_sem, peer_send, peer_recv):
    rep = lax.axis_index('rep')
    row = lax.axis_index('rows')
    z, y, x = lax.div(row, 16), lax.rem(lax.div(row, 4), 4), lax.rem(row, 4)
    zr = lax.rem(z + 4 - 2 * rep, 4)
    is_src = zr < 2
    near = lax.div(lax.rem(zr + 1, 4), 2)
    inward = 1 - 2 * near
    xs = [lax.rem(x + d, 4) for d in range(4)]
    ys = [lax.rem(y + d, 4) for d in range(4)]
    planes = [near * 48, 48 - near * 48]
    grid = [[[planes[zc] + ys[dy] * 12 + xs[dx] * 3 for dx in range(4)] for dy in range(4)] for zc in range(2)]

    def rows_at(axis, d):
        if axis == 'x':
            return z * 16 + y * 4 + xs[d % 4]
        if axis == 'y':
            return z * 16 + ys[d % 4] * 4 + x
        return lax.rem(z + d * inward + 4, 4) * 16 + y * 4 + x

    links = [('x', 1), ('x', -1), ('y', 1), ('y', -1), ('z', 1), ('z', -1)]
    target = {link: rows_at(*link) for link in links}

    barrier = pltpu.get_barrier_semaphore()
    for link in links:
        pl.semaphore_signal(barrier, inc=1, device_id=(rep, target[link]), device_id_type=MESH)
    pl.semaphore_signal(barrier, inc=1, device_id=(1 - rep, row), device_id_type=MESH)

    loads = [(h0, h0_v), (w1, w1_v), (w2, w2_v), (adj, a_v)]
    loads = [pltpu.make_async_copy(src, dst, load_sem.at[i]) for i, (src, dst) in enumerate(loads)]
    for copy in loads:
        copy.start()

    def slot_of(word):
        p, zc, dy, dx = word
        return grid[zc][dy][dx] + p

    def send_piece(layer, tab, recv_sem, src_role, word):
        slot = slot_of(word)
        for link in piece_sends(src_role, *word):
            pltpu.make_async_remote_copy(
                src_ref=tab.at[slot], dst_ref=tab.at[slot],
                send_sem=send_sem.at[layer, 'xyz'.index(link[0])], recv_sem=recv_sem.at[slot],
                device_id=(rep, target[link]), device_id_type=MESH).start()

    def wait_piece(tab, recv_sem, word):
        slot = slot_of(word)
        pltpu.make_async_copy(tab.at[slot], tab.at[slot], recv_sem.at[slot]).wait()

    own = [(p, 0, 0, 0) for p in range(3)]

    loads[0].wait()

    @pl.when(is_src)
    def _():
        for p in range(3):
            part = h0_v[p * PART:(p + 1) * PART, :].astype(jnp.float32)
            tab1[slot_of(own[p])] = part.T.astype(jnp.bfloat16)

    pl.semaphore_wait(barrier, 7)

    @pl.when(is_src)
    def _():
        for p in range(3):
            send_piece(0, tab1, recv_sem1, True, own[p])

    loads[1].wait()
    w1t[...] = w1_v[...].astype(jnp.float32).T.astype(jnp.bfloat16)
    acc1[...] = jnp.zeros_like(acc1)
    acc2[...] = jnp.zeros_like(acc2)

    def chunk_operands(tab, first):
        a_parts, t_parts = [], []
        for n in range(first, first + CHUNK):
            slot = lax.select(is_src, slot_of(SRC_ORDER[n]), slot_of(SINK_ORDER[n]))
            keep = mask[row, rep * 32 + lax.div(slot, 3)].astype(jnp.float32).astype(jnp.bfloat16)
            a_parts.append(a_v[:, pl.ds(pl.multiple_of(slot * PART, PART), PART)])
            t_parts.append(tab[slot] * keep)
        return jnp.concatenate(a_parts, axis=1), jnp.concatenate(t_parts, axis=1)

    def gather(layer, tab, recv_sem, multiply):
        for first in range(0, SLOTS, CHUNK):
            @pl.when(is_src)
            def _():
                for n in range(first, first + CHUNK):
                    if SRC_ORDER[n] not in own:
                        wait_piece(tab, recv_sem, SRC_ORDER[n])
                        send_piece(layer, tab, recv_sem, True, SRC_ORDER[n])

            @pl.when(jnp.logical_not(is_src))
            def _():
                for n in range(first, first + CHUNK):
                    wait_piece(tab, recv_sem, SINK_ORDER[n])
                    send_piece(layer, tab, recv_sem, False, SINK_ORDER[n])

            if layer == 0 and first == 0:
                loads[3].wait()
            multiply(*chunk_operands(tab, first))

    def multiply1(a, t):
        acc1[...] += lax.dot_general(a, t, (((1,), (1,)), ((), ())), preferred_element_type=jnp.float32)

    def multiply2(a, t):
        zt = jnp.dot(w1t[...], t, preferred_element_type=jnp.float32)
        zt = jnp.maximum(zt, 0.0).astype(jnp.bfloat16)
        acc2[...] += lax.dot_general(a, zt, (((1,), (1,)), ((), ())), preferred_element_type=jnp.float32)

    def to_peer(layer, src, dst):
        return pltpu.make_async_remote_copy(
            src_ref=src, dst_ref=dst, send_sem=peer_send.at[layer], recv_sem=peer_recv.at[layer],
            device_id=(1 - rep, row), device_id_type=MESH)

    gather(0, tab1, recv_sem1, multiply1)
    swap1 = to_peer(0, acc1, peer1)

    @pl.when(jnp.logical_not(is_src))
    def _():
        swap1.start()

    @pl.when(is_src)
    def _():
        swap1.wait_recv()
        for p in range(3):
            rows = slice(p * PART, (p + 1) * PART)
            part = acc1[rows, :] + peer1[rows, :]
            tab2[slot_of(own[p])] = part.T.astype(jnp.bfloat16)
        for p in range(3):
            send_piece(1, tab2, recv_sem2, True, own[p])

    gather(1, tab2, recv_sem2, multiply2)
    swap2 = to_peer(1, acc2, peer2)
    swap2.start()
    loads[2].wait()
    swap2.wait_recv()
    y_two = (acc2[...] + peer2[...]).astype(jnp.bfloat16)
    out[...] = jnp.dot(y_two, w2_v[...], preferred_element_type=jnp.float32)

    def drain(role):
        for layer, tab in ((0, tab1), (1, tab2)):
            for i, axis in enumerate('xyz'):
                words = SRC_ORDER if role else SINK_ORDER
                count = sum(link[0] == axis for word in words for link in piece_sends(role, *word))
                ref = tab.at[pl.ds(0, count)]
                pltpu.make_async_copy(ref, ref, send_sem.at[layer, i]).wait()

    @pl.when(is_src)
    def _():
        drain(True)

    @pl.when(jnp.logical_not(is_src))
    def _():
        drain(False)
        swap1.wait_send()

    swap2.wait_send()


def solution(mesh):
    def step(adj, mask, h0, w1, w2):
        any_space = pl.BlockSpec(memory_space=pl.ANY)
        return pl.pallas_call(
            kernel,
            name='gcn',
            out_shape=jax.ShapeDtypeStruct((BLOCK, F2), jnp.float32),
            in_specs=[any_space, pl.BlockSpec(memory_space=pltpu.SMEM), any_space, any_space, any_space],
            out_specs=pl.BlockSpec(memory_space=pltpu.VMEM),
            scratch_shapes=[
                pltpu.VMEM((BLOCK, 32 * BLOCK), jnp.bfloat16),
                pltpu.VMEM((BLOCK, F0), jnp.bfloat16),
                pltpu.VMEM((F0, F1), jnp.bfloat16),
                pltpu.VMEM((F1, F0), jnp.bfloat16),
                pltpu.VMEM((F1, F2), jnp.bfloat16),
                pltpu.VMEM((SLOTS, F0, PART), jnp.bfloat16),
                pltpu.VMEM((SLOTS, F0, PART), jnp.bfloat16),
                pltpu.VMEM((BLOCK, F0), jnp.float32),
                pltpu.VMEM((BLOCK, F1), jnp.float32),
                pltpu.VMEM((BLOCK, F0), jnp.float32),
                pltpu.VMEM((BLOCK, F1), jnp.float32),
                pltpu.SemaphoreType.DMA((4,)),
                pltpu.SemaphoreType.DMA((SLOTS,)),
                pltpu.SemaphoreType.DMA((SLOTS,)),
                pltpu.SemaphoreType.DMA((2, 3)),
                pltpu.SemaphoreType.DMA((2,)),
                pltpu.SemaphoreType.DMA((2,)),
            ],
            compiler_params=pltpu.CompilerParams(
                collective_id=0, has_side_effects=True, vmem_limit_bytes=60 * 1024 * 1024),
        )(adj, mask, h0, w1, w2)

    return jax.shard_map(step, mesh=mesh, in_specs=(P('rows', 'rep'), P(), P('rows', None), P(), P()),
                         out_specs=P('rows', None), check_vma=False)
```

time: 215 us -> 84.1 us (0.39)
  waiting for transfers between devices: 157 us -> 0 us
  Pallas kernels: 0 us -> 77.4 us
  matrix products: 20.9 us -> 0 us
  between operations: 13.5 us -> 0.01 us
  blocking collectives: 12.1 us -> 0 us
  starting transfers between devices: 7.62 us -> 0 us
  local copies, waits for them, and re-layouts: 2.53 us -> 5.12 us
    all_gather x2 -> x0, waiting for transfers between devices: 148 us -> none  [range_rows(): return lax.all_gather(recv_piece, 'rows', axis=0, tiled=True)]
    pallas_call x0 -> x1, Pallas kernels: none -> 77.4 us  [step(): pl.pallas_call(kernel, name='gcn', out_shape=jax.ShapeDtypeStruct((BLOCK,...]
    dot_general x3 -> x0, matrix products: 20.9 us -> none  [the longest x2 20 us: aggregate(): part_sum = jnp.dot(adj_local, masked, preferred_element_type=jnp.float32)]
    psum x2 -> x0, blocking collectives: 12.1 us -> none  [aggregate(): return lax.psum(part_sum, 'rep').astype(jnp.bfloat16)]
    ppermute x2 -> x0, waiting for transfers between devices: 9.05 us -> none  [range_rows(): recv_piece = lax.ppermute(send_piece, ('rep', 'rows'), perm_pairs)]
    ppermute x2 -> x0, starting transfers between devices: 7.58 us -> none  [range_rows(): recv_piece = lax.ppermute(send_piece, ('rep', 'rows'), perm_pairs)]
  transfers between devices with their start and end apart: 4 -> 0, of which waited for: 4 -> 0; matrix products, arithmetic and copies ran while one was open for 0% -> 0% of each run, Pallas kernels for 0% -> 0%
where the time goes in v2:
time: 84.1 us; the launch traced here: 82.5 us
  Pallas kernels  77.4 us (92%)
  local copies, waits for them, and re-layouts  5.12 us (6%)
    pallas_call x1, Pallas kernels, step(): pl.pallas_call(kernel, name='gcn', out_shape=jax.ShapeDtypeStruct((BLOCK,...  77.4 us
    unnamed x2, local copies, waits for them, and re-layouts  3.39 us
    pallas_call x1, local copies, waits for them, and re-layouts, step(): pl.pallas_call(kernel, name='gcn', out_shape=jax.ShapeDtypeStruct((BLOCK,...  1.73 us

profile of v2, /device:TPU:1, one launch (start us, length us, event | category | flops | bytes accessed | tf_op | source)
XLA Modules:
  0.0 82.5 jit_solution(4043100731601323779)
XLA Ops:
  0.0 1.7 %copy.7.w2 = bf16[512,107]{1,0:T(8,128)(2,1)} copy(bf16[512,107]{0,1:T(8,128)(2,1)} %param.9) | data formatting | bytes 219136 | tf_op args[4]
  1.7 1.7 %copy.6.h0 = bf16[384,200]{1,0:T(8,128)(2,1)} copy(bf16[384,200]{0,1:T(8,128)(2,1)} %param.7) | data formatting | bytes 307200 | tf_op args[2]
  3.4 77.4 %gcn.1 = f32[384,107]{1,0:T(8,128)} custom-call(bf16[384,12288]{1,0:T(8,128)(2,1)} %adj.1, s32[64,64]{1,0:T(8,128)} %mask.1, bf16[384,200]{1,0:T(8,128)(2,1)} %copy.6.h0, bf16[200,512]{1,0:T(8,128)(2,1)} %w1.1, bf16[512,107]{1,0:T(8,128)(2,1)} %copy.7.w2), custom_call_target="tpu_custom_call" | custom-call | tf_op jit(solution)/shard_map/gcn/pallas_call | solution.py:229
  80.8 1.7 %copy.8 = f32[384,107]{0,1:T(8,128)} copy(f32[384,107]{1,0:T(8,128)} %gcn.1) | data formatting | bytes 328704 | tf_op jit(solution)/shard_map/gcn/pallas_call | solution.py:229

commit v3 on v2

v3 whole, which is shorter than its diff:
```python
import heapq
import itertools

import jax
import jax.numpy as jnp
from jax import lax
from jax.experimental import pallas as pl
from jax.experimental.pallas import tpu as pltpu
from jax.sharding import PartitionSpec as P

BLOCK = 384
F0, F1, F2 = 200, 512, 107
PART = 128
SLOTS = 96
CHUNK = 4
BAND = 32
LEAD = 6
AXES = ('xyz', 'yzx', 'zxy')
MESH = pl.DeviceIdType.MESH
MODEL = 0.55, 1.6, 0.1


def relay_bit(p, axis, off):
    before = AXES[p][:AXES[p].index(axis)]
    return sum(off[a] for a in before) % 2


def piece_sends(is_src, p, zc, dy, dx):
    off = {'x': dx, 'y': dy, 'z': zc}
    order = AXES[p]
    last = -1
    for i, a in enumerate(order):
        if (off[a] != 0) if a != 'z' else (not is_src or zc == 1):
            last = i
    out = []
    if last >= 0:
        a = order[last]
        bit = relay_bit(p, a, off)
        if a in 'xy':
            if off[a] == 3 and bit == 0:
                out.append((a, 1))
            if off[a] == 1 and bit == 1:
                out.append((a, -1))
        elif is_src and zc == 1 and bit == 0:
            out.append(('z', -1))
        elif not is_src and zc == 0 and bit == 1:
            out.append(('z', -1))
    for a in order[last + 1:]:
        out += [(a, 1), (a, -1)]
    return out


def core_roles():
    roles = {}
    for rep, z, y, x in itertools.product(range(2), range(4), range(4), range(4)):
        zr = (z - 2 * rep) % 4
        near = (zr + 1) % 4 // 2
        roles[rep, z, y, x] = zr < 2, near, 1 - 2 * near
    return roles


def arrival_orders():
    roles = core_roles()
    piece_time, hop_time, turn_time = MODEL
    orders = None
    for _ in range(4):
        arrived = {core: {} for core in roles}
        link_free, clock, place = {}, {}, {}
        events, tick = [], itertools.count()

        def word_of(core, piece):
            p, plane, sy, sx = piece
            return p, int(plane != roles[core][1]), (sy - core[2]) % 4, (sx - core[3]) % 4

        def send(core, piece, now):
            rep, z, y, x = core
            is_src, _, inward = roles[core]
            for axis, d in piece_sends(is_src, *word_of(core, piece)):
                step = d * inward if axis == 'z' else d
                to = {'x': (rep, z, y, (x + step) % 4), 'y': (rep, z, (y + step) % 4, x), 'z': (rep, (z + step) % 4, y, x)}[axis]
                link = z, y, x, axis, step
                link_free[link] = max(now, link_free.get(link, 0.0)) + piece_time
                heapq.heappush(events, (link_free[link] + hop_time, next(tick), to, piece))

        def advance(core, now):
            if orders is None:
                return
            is_src, near, _ = roles[core]
            words = orders[is_src]
            while place[core] < SLOTS:
                p, zc, dy, dx = words[place[core]]
                piece = p, near ^ zc, (core[2] + dy) % 4, (core[3] + dx) % 4
                if piece not in arrived[core]:
                    return
                start = max(clock[core], arrived[core][piece])
                if start > now:
                    heapq.heappush(events, (start, next(tick), core, None))
                    return
                place[core] += 1
                clock[core] = start + (turn_time if place[core] % CHUNK == 0 else 0.0)
                send(core, piece, start)

        for core, (is_src, near, _) in roles.items():
            place[core], clock[core] = 0, 0.0
            for p in range(3 if is_src else 0):
                piece = p, near, core[2], core[3]
                arrived[core][piece] = 0.0
                if orders is None:
                    send(core, piece, 0.0)
            advance(core, 0.0)
        while events:
            now, _, core, piece = heapq.heappop(events)
            if piece is not None:
                arrived[core][piece] = now
                if orders is None:
                    send(core, piece, now)
            advance(core, now)
        times = {True: {}, False: {}}
        for core in roles:
            for piece, now in arrived[core].items():
                times[roles[core][0]].setdefault(word_of(core, piece), []).append(now)
        orders = {role: sorted(t, key=lambda w: (sum(t[w]) / len(t[w]), w)) for role, t in times.items()}
    return orders[True], orders[False], max(max(t.values()) for t in arrived.values())


SRC_ORDER, SINK_ORDER, _ = arrival_orders()


def kernel(adj, mask, h0t, w1, w2t, out, a_v, w1_v, w1t, w2t_v, tab1, tab2, acc1, acc2, peer1, peer2,
           load_sem, adj_sem, own_sem, recv_sem1, recv_sem2, send_sem, peer_send, peer_recv):
    rep = lax.axis_index('rep')
    row = lax.axis_index('rows')
    z, y, x = lax.div(row, 16), lax.rem(lax.div(row, 4), 4), lax.rem(row, 4)
    zr = lax.rem(z + 4 - 2 * rep, 4)
    is_src = zr < 2
    near = lax.div(lax.rem(zr + 1, 4), 2)
    inward = 1 - 2 * near
    xs = [lax.rem(x + d, 4) for d in range(4)]
    ys = [lax.rem(y + d, 4) for d in range(4)]
    planes = [near * 48, 48 - near * 48]
    grid = [[[planes[zc] + ys[dy] * 12 + xs[dx] * 3 for dx in range(4)] for dy in range(4)] for zc in range(2)]

    def rows_at(axis, d):
        if axis == 'x':
            return z * 16 + y * 4 + xs[d % 4]
        if axis == 'y':
            return z * 16 + ys[d % 4] * 4 + x
        return lax.rem(z + d * inward + 4, 4) * 16 + y * 4 + x

    links = [('x', 1), ('x', -1), ('y', 1), ('y', -1), ('z', 1), ('z', -1)]
    target = {link: rows_at(*link) for link in links}

    barrier = pltpu.get_barrier_semaphore()
    for link in links:
        pl.semaphore_signal(barrier, inc=1, device_id=(rep, target[link]), device_id_type=MESH)
    pl.semaphore_signal(barrier, inc=1, device_id=(1 - rep, row), device_id_type=MESH)

    loads = [pltpu.make_async_copy(src, dst, load_sem.at[i]) for i, (src, dst) in enumerate([(w1, w1_v), (w2t, w2t_v)])]
    bands = [pl.ds(i * BAND, BAND) for i in range(BLOCK // BAND)]
    adj_loads = [pltpu.make_async_copy(adj.at[rows], a_v.at[rows], adj_sem.at[i]) for i, rows in enumerate(bands)]

    def slot_of(word):
        p, zc, dy, dx = word
        return grid[zc][dy][dx] + p

    def send_piece(layer, tab, recv_sem, src_role, word):
        slot = slot_of(word)
        for link in piece_sends(src_role, *word):
            pltpu.make_async_remote_copy(
                src_ref=tab.at[slot], dst_ref=tab.at[slot],
                send_sem=send_sem.at[layer, 'xyz'.index(link[0])], recv_sem=recv_sem.at[slot],
                device_id=(rep, target[link]), device_id_type=MESH).start()

    def wait_piece(tab, recv_sem, word):
        slot = slot_of(word)
        pltpu.make_async_copy(tab.at[slot], tab.at[slot], recv_sem.at[slot]).wait()

    own = [(p, 0, 0, 0) for p in range(3)]

    own_loads = [pltpu.make_async_copy(h0t.at[:, pl.ds(p * PART, PART)], tab1.at[slot_of(own[p])], own_sem.at[p]) for p in range(3)]

    @pl.when(is_src)
    def _():
        for copy in own_loads:
            copy.start()

    for copy in loads + adj_loads:
        copy.start()

    @pl.when(is_src)
    def _():
        for copy in own_loads:
            copy.wait()

    pl.semaphore_wait(barrier, 7)

    @pl.when(is_src)
    def _():
        for p in range(3):
            send_piece(0, tab1, recv_sem1, True, own[p])

    loads[0].wait()
    w1t[...] = w1_v[...].astype(jnp.float32).T.astype(jnp.bfloat16)
    acc1[...] = jnp.zeros_like(acc1)
    acc2[...] = jnp.zeros_like(acc2)

    def chunk_operands(tab, first):
        a_parts, t_parts = [], []
        for n in range(first, first + CHUNK):
            slot = lax.select(is_src, slot_of(SRC_ORDER[n]), slot_of(SINK_ORDER[n]))
            keep = mask[row, rep * 32 + lax.div(slot, 3)].astype(jnp.float32).astype(jnp.bfloat16)
            a_parts.append(a_v[:, pl.ds(pl.multiple_of(slot * PART, PART), PART)])
            t_parts.append(tab[slot] * keep)
        return jnp.concatenate(a_parts, axis=1), jnp.concatenate(t_parts, axis=1)

    def relay(layer, tab, recv_sem, chunk):
        words = range(chunk * CHUNK, (chunk + 1) * CHUNK)

        @pl.when(is_src)
        def _():
            for n in words:
                if SRC_ORDER[n] not in own:
                    wait_piece(tab, recv_sem, SRC_ORDER[n])
                    send_piece(layer, tab, recv_sem, True, SRC_ORDER[n])

        @pl.when(jnp.logical_not(is_src))
        def _():
            for n in words:
                wait_piece(tab, recv_sem, SINK_ORDER[n])
                send_piece(layer, tab, recv_sem, False, SINK_ORDER[n])

    def gather(layer, tab, recv_sem, multiply, lead):
        done = 0
        for chunk in range(SLOTS // CHUNK):
            relay(layer, tab, recv_sem, chunk)
            if chunk + 1 < lead:
                continue
            if layer == 0 and done == 0:
                for copy in adj_loads:
                    copy.wait()
            for _ in range(2):
                if done <= chunk:
                    multiply(*chunk_operands(tab, done * CHUNK))
                    done += 1

    def multiply1(a, t):
        acc1[...] += lax.dot_general(a, t, (((1,), (1,)), ((), ())), preferred_element_type=jnp.float32)

    def multiply2(a, t):
        zt = jnp.dot(w1t[...], t, preferred_element_type=jnp.float32)
        zt = jnp.maximum(zt, 0.0).astype(jnp.bfloat16)
        acc2[...] += lax.dot_general(a, zt, (((1,), (1,)), ((), ())), preferred_element_type=jnp.float32)

    def to_peer(layer, src, dst):
        return pltpu.make_async_remote_copy(
            src_ref=src, dst_ref=dst, send_sem=peer_send.at[layer], recv_sem=peer_recv.at[layer],
            device_id=(1 - rep, row), device_id_type=MESH)

    gather(0, tab1, recv_sem1, multiply1, LEAD)
    swap1 = to_peer(0, acc1, peer1)

    @pl.when(jnp.logical_not(is_src))
    def _():
        swap1.start()

    @pl.when(is_src)
    def _():
        swap1.wait_recv()
        for p in range(3):
            rows = slice(p * PART, (p + 1) * PART)
            part = acc1[rows, :] + peer1[rows, :]
            tab2[slot_of(own[p])] = part.T.astype(jnp.bfloat16)
        for p in range(3):
            send_piece(1, tab2, recv_sem2, True, own[p])

    gather(1, tab2, recv_sem2, multiply2, 1)
    swap2 = to_peer(1, acc2, peer2)
    swap2.start()
    loads[1].wait()
    swap2.wait_recv()
    y_two = (acc2[...] + peer2[...]).astype(jnp.bfloat16)
    out[...] = lax.dot_general(w2t_v[...], y_two, (((1,), (1,)), ((), ())), preferred_element_type=jnp.float32)

    def drain(role):
        for layer, tab in ((0, tab1), (1, tab2)):
            for i, axis in enumerate('xyz'):
                words = SRC_ORDER if role else SINK_ORDER
                count = sum(link[0] == axis for word in words for link in piece_sends(role, *word))
                ref = tab.at[pl.ds(0, count)]
                pltpu.make_async_copy(ref, ref, send_sem.at[layer, i]).wait()

    @pl.when(is_src)
    def _():
        drain(True)

    @pl.when(jnp.logical_not(is_src))
    def _():
        drain(False)
        swap1.wait_send()

    swap2.wait_send()


def solution(mesh):
    def step(adj, mask, h0, w1, w2):
        h0t, w2t = h0.T, w2.T
        any_space = pl.BlockSpec(memory_space=pl.ANY)
        return pl.pallas_call(
            kernel,
            name='gcn',
            out_shape=jax.ShapeDtypeStruct((F2, BLOCK), jnp.float32),
            in_specs=[any_space, pl.BlockSpec(memory_space=pltpu.SMEM), any_space, any_space, any_space],
            out_specs=pl.BlockSpec(memory_space=pltpu.VMEM),
            scratch_shapes=[
                pltpu.VMEM((BLOCK, 32 * BLOCK), jnp.bfloat16),
                pltpu.VMEM((F0, F1), jnp.bfloat16),
                pltpu.VMEM((F1, F0), jnp.bfloat16),
                pltpu.VMEM((F2, F1), jnp.bfloat16),
                pltpu.VMEM((SLOTS, F0, PART), jnp.bfloat16),
                pltpu.VMEM((SLOTS, F0, PART), jnp.bfloat16),
                pltpu.VMEM((BLOCK, F0), jnp.float32),
                pltpu.VMEM((BLOCK, F1), jnp.float32),
                pltpu.VMEM((BLOCK, F0), jnp.float32),
                pltpu.VMEM((BLOCK, F1), jnp.float32),
                pltpu.SemaphoreType.DMA((2,)),
                pltpu.SemaphoreType.DMA((BLOCK // BAND,)),
                pltpu.SemaphoreType.DMA((3,)),
                pltpu.SemaphoreType.DMA((SLOTS,)),
                pltpu.SemaphoreType.DMA((SLOTS,)),
                pltpu.SemaphoreType.DMA((2, 3)),
                pltpu.SemaphoreType.DMA((2,)),
                pltpu.SemaphoreType.DMA((2,)),
            ],
            compiler_params=pltpu.CompilerParams(
                collective_id=0, has_side_effects=True, vmem_limit_bytes=60 * 1024 * 1024),
        )(adj, mask, h0t, w1, w2t).T

    return jax.shard_map(step, mesh=mesh, in_specs=(P('rows', 'rep'), P(), P('rows', None), P(), P()),
                         out_specs=P('rows', None), check_vma=False)
```

time: 84.1 us -> 77.4 us (0.920); the launches traced: 82.5 us -> 77.1 us
  local copies, waits for them, and re-layouts: 5.12 us -> 1.6 us
  Pallas kernels: 77.4 us -> 75.5 us
    pallas_call x1, Pallas kernels: 77.4 us -> 75.5 us  [step(): pl.pallas_call(kernel, name='gcn', out_shape=jax.ShapeDtypeStruct((F2, BL...]
    unnamed x2 -> x1, local copies, waits for them, and re-layouts: 3.39 us -> 1.6 us
    pallas_call x1 -> x0, local copies, waits for them, and re-layouts: 1.73 us -> none  [step(): pl.pallas_call(kernel, name='gcn', out_shape=jax.ShapeDtypeStruct((BLOCK,...]
where the time goes in v3:
time: 77.4 us; the launch traced here: 77.1 us
  Pallas kernels  75.5 us (98%)
  local copies, waits for them, and re-layouts  1.6 us (2%)
    pallas_call x1, Pallas kernels, step(): pl.pallas_call(kernel, name='gcn', out_shape=jax.ShapeDtypeStruct((F2, BL...  75.5 us
    unnamed x1, local copies, waits for them, and re-layouts  1.6 us

profile of v3, /device:TPU:1, one launch (start us, length us, event | category | flops | bytes accessed | tf_op | source)
XLA Modules:
  0.0 77.1 jit_solution(907269617913544505)
XLA Ops:
  0.0 75.5 %gcn.1 = f32[107,384]{1,0:T(8,128)} custom-call(bf16[384,12288]{1,0:T(8,128)(2,1)} %adj.1, s32[64,64]{1,0:T(8,128)} %mask.1, bf16[200,384]{1,0:T(8,128)(2,1)} %bitcast.4, bf16[200,512]{1,0:T(8,128)(2,1)} %w1.1, bf16[107,512]{1,0:T(8,128)(2,1)} %bitcast.5), custom_call_target="tpu_custom_call" | custom-call | tf_op jit(solution)/shard_map/gcn/pallas_call | solution.py:308
  75.5 1.6 %copy.7 = f32[384,107]{0,1:T(8,128)} copy(f32[384,107]{0,1:T(8,128)} %bitcast.3) | data formatting | bytes 328704

commit v4 on v3

--- a/solution.py
+++ b/solution.py
@@ -1,6 +1,3 @@
-import heapq
-import itertools
-
 import jax
 import jax.numpy as jnp
 from jax import lax
@@ -17,7 +14,6 @@
 LEAD = 6
 AXES = ('xyz', 'yzx', 'zxy')
 MESH = pl.DeviceIdType.MESH
-MODEL = 0.55, 1.6, 0.1
 
 
 def relay_bit(p, axis, off):
@@ -50,80 +46,23 @@
     return out
 
 
-def core_roles():
-    roles = {}
-    for rep, z, y, x in itertools.product(range(2), range(4), range(4), range(4)):
-        zr = (z - 2 * rep) % 4
-        near = (zr + 1) % 4 // 2
-        roles[rep, z, y, x] = zr < 2, near, 1 - 2 * near
-    return roles
-
-
-def arrival_orders():
-    roles = core_roles()
-    piece_time, hop_time, turn_time = MODEL
-    orders = None
-    for _ in range(4):
-        arrived = {core: {} for core in roles}
-        link_free, clock, place = {}, {}, {}
-        events, tick = [], itertools.count()
-
-        def word_of(core, piece):
-            p, plane, sy, sx = piece
-            return p, int(plane != roles[core][1]), (sy - core[2]) % 4, (sx - core[3]) % 4
-
-        def send(core, piece, now):
-            rep, z, y, x = core
-            is_src, _, inward = roles[core]
-            for axis, d in piece_sends(is_src, *word_of(core, piece)):
-                step = d * inward if axis == 'z' else d
-                to = {'x': (rep, z, y, (x + step) % 4), 'y': (rep, z, (y + step) % 4, x), 'z': (rep, (z + step) % 4, y, x)}[axis]
-                link = z, y, x, axis, step
-                link_free[link] = max(now, link_free.get(link, 0.0)) + piece_time
-                heapq.heappush(events, (link_free[link] + hop_time, next(tick), to, piece))
-
-        def advance(core, now):
-            if orders is None:
-                return
-            is_src, near, _ = roles[core]
-            words = orders[is_src]
-            while place[core] < SLOTS:
-                p, zc, dy, dx = words[place[core]]
-                piece = p, near ^ zc, (core[2] + dy) % 4, (core[3] + dx) % 4
-                if piece not in arrived[core]:
-                    return
-                start = max(clock[core], arrived[core][piece])
-                if start > now:
-                    heapq.heappush(events, (start, next(tick), core, None))
-                    return
-                place[core] += 1
-                clock[core] = start + (turn_time if place[core] % CHUNK == 0 else 0.0)
-                send(core, piece, start)
-
-        for core, (is_src, near, _) in roles.items():
-            place[core], clock[core] = 0, 0.0
-            for p in range(3 if is_src else 0):
-                piece = p, near, core[2], core[3]
-                arrived[core][piece] = 0.0
-                if orders is None:
-                    send(core, piece, 0.0)
-            advance(core, 0.0)
-        while events:
-            now, _, core, piece = heapq.heappop(events)
-            if piece is not None:
-                arrived[core][piece] = now
-                if orders is None:
-                    send(core, piece, now)
-            advance(core, now)
-        times = {True: {}, False: {}}
-        for core in roles:
-            for piece, now in arrived[core].items():
-                times[roles[core][0]].setdefault(word_of(core, piece), []).append(now)
-        orders = {role: sorted(t, key=lambda w: (sum(t[w]) / len(t[w]), w)) for role, t in times.items()}
-    return orders[True], orders[False], max(max(t.values()) for t in arrived.values())
-
-
-SRC_ORDER, SINK_ORDER, _ = arrival_orders()
+def words(codes):
+    return [(c // 32, c // 16 % 2, c // 4 % 4, c % 4) for c in codes]
+
+
+SRC_CODES = [
+    0, 32, 64, 80, 1, 3, 36, 44, 48, 4, 12, 65, 67, 16, 33, 35, 68, 76, 60, 81, 2, 7, 40, 83,
+    84, 52, 5, 45, 15, 19, 92, 13, 37, 66, 17, 8, 49, 71, 47, 28, 69, 20, 39, 79, 82, 51, 77, 56,
+    14, 6, 11, 9, 72, 34, 18, 61, 23, 53, 87, 31, 85, 41, 21, 88, 63, 95, 46, 29, 10, 93, 38, 55,
+    43, 70, 24, 50, 78, 75, 73, 30, 59, 22, 94, 27, 25, 57, 86, 62, 91, 89, 26, 54, 42, 74, 58, 90,
+]
+SINK_CODES = [
+    64, 32, 0, 65, 80, 67, 44, 68, 36, 48, 33, 76, 3, 1, 35, 81, 83, 12, 60, 40, 66, 4, 52, 16,
+    84, 45, 69, 2, 37, 7, 71, 82, 92, 47, 56, 49, 15, 77, 79, 5, 39, 51, 13, 72, 19, 8, 17, 34,
+    87, 61, 41, 85, 28, 14, 63, 43, 70, 20, 95, 6, 53, 11, 93, 55, 78, 9, 18, 46, 88, 23, 38, 73,
+    59, 94, 75, 31, 57, 50, 86, 21, 29, 30, 10, 22, 27, 91, 62, 42, 89, 24, 25, 74, 54, 58, 90, 26,
+]
+SRC_ORDER, SINK_ORDER = words(SRC_CODES), words(SINK_CODES)
 
 
 def kernel(adj, mask, h0t, w1, w2t, out, a_v, w1_v, w1t, w2t_v, tab1, tab2, acc1, acc2, peer1, peer2,

time: 77.4 us -> 70.1 us (0.906)
  Pallas kernels: 75.5 us -> 68.3 us
    pallas_call x1, Pallas kernels: 75.5 us -> 68.3 us  [step(): pl.pallas_call(kernel, name='gcn', out_shape=jax.ShapeDtypeStruct((F2, BL...]
where the time goes in v4:
time: 70.1 us; the launch traced here: 69.9 us
  Pallas kernels  68.3 us (97%)
  local copies, waits for them, and re-layouts  1.6 us (2%)
    pallas_call x1, Pallas kernels, step(): pl.pallas_call(kernel, name='gcn', out_shape=jax.ShapeDtypeStruct((F2, BL...  68.3 us
    unnamed x1, local copies, waits for them, and re-layouts  1.6 us

profile of v4, /device:TPU:1, one launch (start us, length us, event | category | flops | bytes accessed | tf_op | source)
XLA Modules:
  0.0 69.9 jit_solution(1249604551256214301)
XLA Ops:
  0.0 68.3 %gcn.1 = f32[107,384]{1,0:T(8,128)} custom-call(bf16[384,12288]{1,0:T(8,128)(2,1)} %adj.1, s32[64,64]{1,0:T(8,128)} %mask.1, bf16[200,384]{1,0:T(8,128)(2,1)} %bitcast.4, bf16[200,512]{1,0:T(8,128)(2,1)} %w1.1, bf16[107,512]{1,0:T(8,128)(2,1)} %bitcast.5), custom_call_target="tpu_custom_call" | custom-call | tf_op jit(solution)/shard_map/gcn/pallas_call | solution.py:247
  68.3 1.6 %copy.7 = f32[384,107]{0,1:T(8,128)} copy(f32[384,107]{0,1:T(8,128)} %bitcast.3) | data formatting | bytes 328704

commit v5 on v4

v5 whole, which is shorter than its diff:
```python
import jax
import jax.numpy as jnp
from jax import lax
from jax.experimental import pallas as pl
from jax.experimental.pallas import tpu as pltpu
from jax.sharding import PartitionSpec as P

BLOCK = 384
F0, F1, F2 = 200, 512, 107
PART = 128
SLOTS = 96
CHUNKS = 8, 4
BAND = 32
DIRECT = 9, 9, 4
LEAD = 24
AXES = ('xyz', 'yzx', 'zxy')
MESH = pl.DeviceIdType.MESH


def relay_bit(p, axis, off):
    before = AXES[p][:AXES[p].index(axis)]
    return sum(off[a] for a in before) % 2


def piece_sends(is_src, p, zc, dy, dx):
    off = {'x': dx, 'y': dy, 'z': zc}
    order = AXES[p]
    last, depth, direct = -1, 0, []
    for i, a in enumerate(order):
        direct.append(depth >= DIRECT[i])
        steps = (zc if is_src else 1 + zc) if a == 'z' else (0, 1, 2, 1)[off[a]]
        if steps:
            last = i
            depth += 1 if direct[i] else steps
    out = []
    if last >= 0 and not direct[last]:
        a = order[last]
        bit = relay_bit(p, a, off)
        if a in 'xy':
            if off[a] == 3 and bit == 0:
                out.append((a, 1))
            if off[a] == 1 and bit == 1:
                out.append((a, -1))
        elif is_src and zc == 1 and bit == 0:
            out.append(('z', -1))
        elif not is_src and zc == 0 and bit == 1:
            out.append(('z', -1))
    for i in range(last + 1, 3):
        out += [(order[i], 1), (order[i], -1)] + [(order[i], 2)] * direct[i]
    return out


def words(codes):
    return [(c // 32, c // 16 % 2, c // 4 % 4, c % 4) for c in codes]


SRC_CODES = [
    0, 32, 64, 1, 3, 36, 44, 80, 4, 12, 48, 65, 67, 16, 33, 35, 68, 76, 2, 60, 52, 40, 7, 83,
    84, 13, 5, 81, 15, 17, 19, 37, 45, 66, 92, 8, 39, 28, 20, 49, 69, 71, 34, 79, 51, 14, 56, 77,
    82, 6, 47, 72, 18, 11, 53, 61, 41, 85, 9, 21, 23, 87, 55, 63, 93, 43, 29, 31, 95, 88, 38, 46,
    10, 70, 24, 78, 73, 75, 59, 94, 30, 50, 57, 22, 86, 25, 27, 54, 89, 62, 42, 91, 26, 74, 58, 90,
]
SINK_CODES = [
    64, 32, 0, 80, 65, 67, 44, 36, 68, 48, 76, 1, 3, 4, 12, 35, 83, 81, 92, 40, 66, 60, 52, 16,
    84, 2, 69, 45, 71, 37, 5, 33, 7, 77, 79, 13, 72, 15, 47, 39, 82, 8, 49, 17, 20, 19, 56, 51,
    34, 14, 28, 43, 95, 6, 18, 93, 41, 63, 78, 11, 55, 9, 87, 85, 61, 53, 70, 88, 73, 21, 23, 46,
    38, 75, 94, 29, 31, 59, 50, 57, 86, 30, 42, 91, 10, 24, 89, 22, 90, 62, 26, 54, 74, 25, 27, 58,
]
SRC_ORDER, SINK_ORDER = words(SRC_CODES), words(SINK_CODES)


def kernel(adj, mask_h, h0t, w1, out, a_v, mask, w1_v, w1t, tab1, tab2, y_two, acc1, acc2, peer1, peer2,
           load_sem, adj_sem, own_sem, recv_sem1, recv_sem2, send_sem, peer_send, peer_recv):
    rep = lax.axis_index('rep')
    row = lax.axis_index('rows')
    z, y, x = lax.div(row, 16), lax.rem(lax.div(row, 4), 4), lax.rem(row, 4)
    zr = lax.rem(z + 4 - 2 * rep, 4)
    is_src = zr < 2
    near = lax.div(lax.rem(zr + 1, 4), 2)
    inward = 1 - 2 * near
    xs = [lax.rem(x + d, 4) for d in range(4)]
    ys = [lax.rem(y + d, 4) for d in range(4)]
    planes = [near * 48, 48 - near * 48]
    grid = [[[planes[zc] + ys[dy] * 12 + xs[dx] * 3 for dx in range(4)] for dy in range(4)] for zc in range(2)]

    def rows_at(axis, d):
        if axis == 'x':
            return z * 16 + y * 4 + xs[d % 4]
        if axis == 'y':
            return z * 16 + ys[d % 4] * 4 + x
        return lax.rem(z + d * inward + 4, 4) * 16 + y * 4 + x

    links = [(axis, d) for axis in 'xyz' for d in (1, -1, 2)]
    target = {link: rows_at(*link) for link in links}

    barrier = pltpu.get_barrier_semaphore()
    for link in links:
        pl.semaphore_signal(barrier, inc=1, device_id=(rep, target[link]), device_id_type=MESH)
    pl.semaphore_signal(barrier, inc=1, device_id=(1 - rep, row), device_id_type=MESH)

    loads = [pltpu.make_async_copy(src, dst, load_sem.at[i]) for i, (src, dst) in enumerate([(w1, w1_v), (mask_h, mask)])]
    bands = [pl.ds(i * BAND, BAND) for i in range(BLOCK // BAND)]
    adj_loads = [pltpu.make_async_copy(adj.at[rows], a_v.at[rows], adj_sem.at[i]) for i, rows in enumerate(bands)]

    def slot_of(word):
        p, zc, dy, dx = word
        return grid[zc][dy][dx] + p

    def send_piece(layer, tab, recv_sem, src_role, word):
        slot = slot_of(word)
        for link in piece_sends(src_role, *word):
            pltpu.make_async_remote_copy(
                src_ref=tab.at[slot], dst_ref=tab.at[slot],
                send_sem=send_sem.at[layer, 'xyz'.index(link[0])], recv_sem=recv_sem.at[slot],
                device_id=(rep, target[link]), device_id_type=MESH).start()

    def wait_piece(tab, recv_sem, word):
        slot = slot_of(word)
        pltpu.make_async_copy(tab.at[slot], tab.at[slot], recv_sem.at[slot]).wait()

    own = [(p, 0, 0, 0) for p in range(3)]

    own_loads = [pltpu.make_async_copy(h0t.at[:, pl.ds(p * PART, PART)], tab1.at[slot_of(own[p])], own_sem.at[p]) for p in range(3)]

    @pl.when(is_src)
    def _():
        for copy in own_loads:
            copy.start()

    for copy in loads + adj_loads:
        copy.start()

    @pl.when(is_src)
    def _():
        for copy in own_loads:
            copy.wait()

    pl.semaphore_wait(barrier, len(links) + 1)

    @pl.when(is_src)
    def _():
        for p in range(3):
            send_piece(0, tab1, recv_sem1, True, own[p])

    loads[0].wait()
    w1t[...] = w1_v[...].astype(jnp.float32).T.astype(jnp.bfloat16)
    acc1[...] = jnp.zeros_like(acc1)
    acc2[...] = jnp.zeros_like(acc2)

    def chunk_operands(tab, first, count):
        a_parts, t_parts = [], []
        for n in range(first, first + count):
            slot = lax.select(is_src, slot_of(SRC_ORDER[n]), slot_of(SINK_ORDER[n]))
            keep = mask[row, rep * 32 + lax.div(slot, 3)].astype(jnp.float32).astype(jnp.bfloat16)
            a_parts.append(a_v[:, pl.ds(pl.multiple_of(slot * PART, PART), PART)])
            t_parts.append(tab[slot] * keep)
        return jnp.concatenate(a_parts, axis=1), jnp.concatenate(t_parts, axis=1)

    def relay(layer, tab, recv_sem, words):

        @pl.when(is_src)
        def _():
            for n in words:
                if SRC_ORDER[n] not in own:
                    wait_piece(tab, recv_sem, SRC_ORDER[n])
                    send_piece(layer, tab, recv_sem, True, SRC_ORDER[n])

        @pl.when(jnp.logical_not(is_src))
        def _():
            for n in words:
                wait_piece(tab, recv_sem, SINK_ORDER[n])
                send_piece(layer, tab, recv_sem, False, SINK_ORDER[n])

    def gather(layer, tab, recv_sem, multiply, count, lead):
        done = 0
        for first in range(0, SLOTS, count):
            relay(layer, tab, recv_sem, range(first, first + count))
            if first + count < lead:
                continue
            if layer == 0 and done == 0:
                loads[1].wait()
                for copy in adj_loads:
                    copy.wait()
            for _ in range(2):
                if done <= first:
                    multiply(*chunk_operands(tab, done, count))
                    done += count

    def multiply1(a, t):
        acc1[...] += lax.dot_general(a, t, (((1,), (1,)), ((), ())), preferred_element_type=jnp.float32)

    def multiply2(a, t):
        zt = jnp.dot(w1t[...], t, preferred_element_type=jnp.float32)
        zt = jnp.maximum(zt, 0.0).astype(jnp.bfloat16)
        acc2[...] += lax.dot_general(a, zt, (((1,), (1,)), ((), ())), preferred_element_type=jnp.float32)

    parts = [slice(p * PART, (p + 1) * PART) for p in range(3)]

    def to_peer(layer, src, dst):
        return [pltpu.make_async_remote_copy(
            src_ref=src.at[pl.ds(p * PART, PART)], dst_ref=dst.at[pl.ds(p * PART, PART)],
            send_sem=peer_send.at[layer, p], recv_sem=peer_recv.at[layer, p],
            device_id=(1 - rep, row), device_id_type=MESH) for p in range(3)]

    gather(0, tab1, recv_sem1, multiply1, CHUNKS[0], LEAD)
    swap1 = to_peer(0, acc1, peer1)

    @pl.when(jnp.logical_not(is_src))
    def _():
        for copy in swap1:
            copy.start()

    @pl.when(is_src)
    def _():
        for p in range(3):
            swap1[p].wait_recv()
            part = acc1[parts[p], :] + peer1[parts[p], :]
            tab2[slot_of(own[p])] = part.T.astype(jnp.bfloat16)
        for p in range(3):
            send_piece(1, tab2, recv_sem2, True, own[p])

    gather(1, tab2, recv_sem2, multiply2, CHUNKS[1], 0)
    swap2 = to_peer(1, acc2, peer2)
    stores = [pltpu.make_async_copy(y_two.at[pl.ds(p * PART, PART)], out.at[pl.ds(p * PART, PART)], own_sem.at[p]) for p in range(3)]
    for copy in swap2:
        copy.start()
    for p in range(3):
        swap2[p].wait_recv()
        y_two[parts[p], :] = (acc2[parts[p], :] + peer2[parts[p], :]).astype(jnp.bfloat16)
        stores[p].start()

    def drain(role):
        for layer, tab in ((0, tab1), (1, tab2)):
            for i, axis in enumerate('xyz'):
                words = SRC_ORDER if role else SINK_ORDER
                count = sum(link[0] == axis for word in words for link in piece_sends(role, *word))
                ref = tab.at[pl.ds(0, count)]
                pltpu.make_async_copy(ref, ref, send_sem.at[layer, i]).wait()

    @pl.when(is_src)
    def _():
        drain(True)

    @pl.when(jnp.logical_not(is_src))
    def _():
        drain(False)
        for copy in swap1:
            copy.wait_send()

    for copy in swap2:
        copy.wait_send()
    for copy in stores:
        copy.wait()


def solution(mesh):
    def step(adj, mask, h0, w1, w2):
        any_space = pl.BlockSpec(memory_space=pl.ANY)
        y_two = pl.pallas_call(
            kernel,
            name='gcn',
            out_shape=jax.ShapeDtypeStruct((BLOCK, F1), jnp.bfloat16),
            in_specs=[any_space] * 4,
            out_specs=any_space,
            scratch_shapes=[
                pltpu.VMEM((BLOCK, 32 * BLOCK), jnp.bfloat16),
                pltpu.SMEM((64, 64), jnp.int32),
                pltpu.VMEM((F0, F1), jnp.bfloat16),
                pltpu.VMEM((F1, F0), jnp.bfloat16),
                pltpu.VMEM((SLOTS, F0, PART), jnp.bfloat16),
                pltpu.VMEM((SLOTS, F0, PART), jnp.bfloat16),
                pltpu.VMEM((BLOCK, F1), jnp.bfloat16),
                pltpu.VMEM((BLOCK, F0), jnp.float32),
                pltpu.VMEM((BLOCK, F1), jnp.float32),
                pltpu.VMEM((BLOCK, F0), jnp.float32),
                pltpu.VMEM((BLOCK, F1), jnp.float32),
                pltpu.SemaphoreType.DMA((2,)),
                pltpu.SemaphoreType.DMA((BLOCK // BAND,)),
                pltpu.SemaphoreType.DMA((3,)),
                pltpu.SemaphoreType.DMA((SLOTS,)),
                pltpu.SemaphoreType.DMA((SLOTS,)),
                pltpu.SemaphoreType.DMA((2, 3)),
                pltpu.SemaphoreType.DMA((2, 3)),
                pltpu.SemaphoreType.DMA((2, 3)),
            ],
            compiler_params=pltpu.CompilerParams(
                collective_id=0, has_side_effects=True, vmem_limit_bytes=60 * 1024 * 1024),
        )(adj, mask, h0.T, w1)
        return jnp.dot(y_two, w2, preferred_element_type=jnp.float32)

    return jax.shard_map(step, mesh=mesh, in_specs=(P('rows', 'rep'), P(), P('rows', None), P(), P()),
                         out_specs=P('rows', None), check_vma=False)
```

time: 70.1 us -> 65.4 us (0.933)
  Pallas kernels: 68.3 us -> 63.3 us
  matrix products: 0 us -> 1.95 us
  local copies, waits for them, and re-layouts: 1.6 us -> 0.01 us
    pallas_call x1, Pallas kernels: 68.3 us -> 63.3 us  [step(): pl.pallas_call(kernel, name='gcn', out_shape=jax.ShapeDtypeStruct((BLOCK,...]
    dot_general x0 -> x1, matrix products: none -> 1.95 us  [step(): return jnp.dot(y_two, w2, preferred_element_type=jnp.float32)]
    unnamed x1 -> x2, local copies, waits for them, and re-layouts: 1.6 us -> 0.01 us
where the time goes in v5:
time: 65.4 us; the launch traced here: 65.2 us
  Pallas kernels  63.3 us (97%)
  matrix products  1.95 us (3%)
    pallas_call x1, Pallas kernels, step(): pl.pallas_call(kernel, name='gcn', out_shape=jax.ShapeDtypeStruct((BLOCK,...  63.3 us
    dot_general x1, matrix products, step(): return jnp.dot(y_two, w2, preferred_element_type=jnp.float32)  1.95 us

profile of v5, /device:TPU:1, one launch (start us, length us, event | category | flops | bytes accessed | tf_op | source)
XLA Modules:
  0.0 65.2 jit_solution(14093436975465520043)
XLA Ops:
  0.0 0.0 copy-start
  0.0 63.3 %gcn.1 = bf16[384,512]{1,0:T(8,128)(2,1)} custom-call(bf16[384,12288]{1,0:T(8,128)(2,1)} %adj.1, s32[64,64]{1,0:T(8,128)} %mask_h.1, bf16[200,384]{1,0:T(8,128)(2,1)} %bitcast.3, bf16[200,512]{1,0:T(8,128)(2,1)} %w1.1), custom_call_target="tpu_custom_call" | custom-call | tf_op jit(solution)/shard_map/gcn/pallas_call | solution.py:259
  63.3 0.0 copy-done
  63.3 2.0 %fusion = f32[384,107]{0,1:T(8,128)} fusion(bf16[384,512]{1,0:T(8,128)(2,1)} %gcn.1, bf16[512,107]{0,1:T(8,128)(2,1)S(1)} %copy-done), kind=kOutput, calls=%fused_computation | convolution fusion | flops 42074112 | bytes 667136 | tf_op jit(solution)/shard_map/dot_general | solution.py:289
Async XLA Ops:
  0.0 63.3 %copy-start = (bf16[512,107]{0,1:T(8,128)(2,1)S(1)}, bf16[512,107]{0,1:T(8,128)(2,1)}, u32[]{:S(2)}) copy-start(bf16[512,107]{0,1:T(8,128)(2,1)} %param.9) | copy-start | bytes 328708

commit v6 on v5

--- a/solution.py
+++ b/solution.py
@@ -55,21 +55,21 @@
 
 
 SRC_CODES = [
-    0, 32, 64, 1, 3, 36, 44, 80, 4, 12, 48, 65, 67, 16, 33, 35, 68, 76, 2, 60, 52, 40, 7, 83,
-    84, 13, 5, 81, 15, 17, 19, 37, 45, 66, 92, 8, 39, 28, 20, 49, 69, 71, 34, 79, 51, 14, 56, 77,
-    82, 6, 47, 72, 18, 11, 53, 61, 41, 85, 9, 21, 23, 87, 55, 63, 93, 43, 29, 31, 95, 88, 38, 46,
-    10, 70, 24, 78, 73, 75, 59, 94, 30, 50, 57, 22, 86, 25, 27, 54, 89, 62, 42, 91, 26, 74, 58, 90,
+    0, 32, 64, 3, 36, 80, 44, 4, 1, 48, 65, 67, 33, 35, 68, 76, 12, 2, 52, 40, 84, 7, 83, 81,
+    60, 13, 5, 15, 16, 17, 37, 45, 66, 92, 8, 39, 20, 49, 69, 18, 71, 19, 34, 79, 51, 14, 11, 56,
+    6, 77, 82, 47, 53, 61, 72, 28, 41, 85, 9, 55, 23, 21, 87, 63, 93, 43, 46, 29, 31, 95, 88, 38,
+    10, 70, 24, 59, 78, 73, 57, 30, 50, 22, 75, 86, 54, 62, 42, 26, 25, 89, 91, 74, 94, 58, 27, 90,
 ]
 SINK_CODES = [
-    64, 32, 0, 80, 65, 67, 44, 36, 68, 48, 76, 1, 3, 4, 12, 35, 83, 81, 92, 40, 66, 60, 52, 16,
-    84, 2, 69, 45, 71, 37, 5, 33, 7, 77, 79, 13, 72, 15, 47, 39, 82, 8, 49, 17, 20, 19, 56, 51,
-    34, 14, 28, 43, 95, 6, 18, 93, 41, 63, 78, 11, 55, 9, 87, 85, 61, 53, 70, 88, 73, 21, 23, 46,
-    38, 75, 94, 29, 31, 59, 50, 57, 86, 30, 42, 91, 10, 24, 89, 22, 90, 62, 26, 54, 74, 25, 27, 58,
+    32, 64, 0, 80, 65, 44, 36, 3, 68, 67, 48, 76, 1, 4, 12, 35, 2, 81, 92, 40, 83, 60, 84, 69,
+    45, 16, 52, 66, 71, 5, 37, 33, 7, 15, 77, 79, 13, 72, 49, 82, 17, 39, 47, 56, 51, 43, 8, 34,
+    28, 14, 95, 6, 63, 93, 20, 41, 78, 55, 11, 19, 9, 87, 85, 53, 70, 21, 23, 73, 88, 18, 46, 38,
+    86, 75, 94, 31, 29, 10, 59, 50, 57, 61, 30, 91, 24, 42, 89, 22, 62, 90, 26, 54, 74, 25, 27, 58,
 ]
 SRC_ORDER, SINK_ORDER = words(SRC_CODES), words(SINK_CODES)
 
 
-def kernel(adj, mask_h, h0t, w1, out, a_v, mask, w1_v, w1t, tab1, tab2, y_two, acc1, acc2, peer1, peer2,
+def kernel(adj, mask_h, h0t, w1, y_two, a_v, mask, w1_v, w1t, tab1, tab2, acc1, acc2, peer1, peer2,
            load_sem, adj_sem, own_sem, recv_sem1, recv_sem2, send_sem, peer_send, peer_recv):
     rep = lax.axis_index('rep')
     row = lax.axis_index('rows')
@@ -221,13 +221,11 @@
 
     gather(1, tab2, recv_sem2, multiply2, CHUNKS[1], 0)
     swap2 = to_peer(1, acc2, peer2)
-    stores = [pltpu.make_async_copy(y_two.at[pl.ds(p * PART, PART)], out.at[pl.ds(p * PART, PART)], own_sem.at[p]) for p in range(3)]
     for copy in swap2:
         copy.start()
     for p in range(3):
         swap2[p].wait_recv()
         y_two[parts[p], :] = (acc2[parts[p], :] + peer2[parts[p], :]).astype(jnp.bfloat16)
-        stores[p].start()
 
     def drain(role):
         for layer, tab in ((0, tab1), (1, tab2)):
@@ -249,19 +247,17 @@
 
     for copy in swap2:
         copy.wait_send()
-    for copy in stores:
-        copy.wait()
 
 
 def solution(mesh):
     def step(adj, mask, h0, w1, w2):
-        any_space = pl.BlockSpec(memory_space=pl.ANY)
+        hbm = pl.BlockSpec(memory_space=pltpu.HBM)
         y_two = pl.pallas_call(
             kernel,
             name='gcn',
             out_shape=jax.ShapeDtypeStruct((BLOCK, F1), jnp.bfloat16),
-            in_specs=[any_space] * 4,
-            out_specs=any_space,
+            in_specs=[hbm] * 4,
+            out_specs=pl.BlockSpec(memory_space=pltpu.VMEM),
             scratch_shapes=[
                 pltpu.VMEM((BLOCK, 32 * BLOCK), jnp.bfloat16),
                 pltpu.SMEM((64, 64), jnp.int32),
@@ -269,7 +265,6 @@
                 pltpu.VMEM((F1, F0), jnp.bfloat16),
                 pltpu.VMEM((SLOTS, F0, PART), jnp.bfloat16),
                 pltpu.VMEM((SLOTS, F0, PART), jnp.bfloat16),
-                pltpu.VMEM((BLOCK, F1), jnp.bfloat16),
                 pltpu.VMEM((BLOCK, F0), jnp.float32),
                 pltpu.VMEM((BLOCK, F1), jnp.float32),
                 pltpu.VMEM((BLOCK, F0), jnp.float32),
@@ -284,8 +279,8 @@
                 pltpu.SemaphoreType.DMA((2, 3)),
             ],
             compiler_params=pltpu.CompilerParams(
-                collective_id=0, has_side_effects=True, vmem_limit_bytes=60 * 1024 * 1024),
-        )(adj, mask, h0.T, w1)
+                collective_id=0, has_side_effects=True, vmem_limit_bytes=40 * 1024 * 1024),
+        )(*[pltpu.with_memory_space_constraint(a, pltpu.HBM) for a in (adj, mask, h0.T, w1)])
         return jnp.dot(y_two, w2, preferred_element_type=jnp.float32)
 
     return jax.shard_map(step, mesh=mesh, in_specs=(P('rows', 'rep'), P(), P('rows', None), P(), P()),

time: 65.4 us -> 64.8 us (level)
  matrix products: 1.95 us -> 0.96 us
    dot_general x1, matrix products: 1.95 us -> 0.96 us  [step(): return jnp.dot(y_two, w2, preferred_element_type=jnp.float32)]
where the time goes in v6:
time: 64.8 us; the launch traced here: 64.7 us
  Pallas kernels  63.7 us (98%)
  matrix products  0.96 us (1%)
    pallas_call x1, Pallas kernels, step(): pl.pallas_call(kernel, name='gcn', out_shape=jax.ShapeDtypeStruct((BLOCK,...  63.7 us

profile of v6, /device:TPU:1, one launch (start us, length us, event | category | flops | bytes accessed | tf_op | source)
XLA Modules:
  0.0 64.7 jit_solution(11482940736311636965)
XLA Ops:
  0.0 0.0 copy-start
  0.0 63.7 %gcn.1 = bf16[384,512]{1,0:T(8,128)(2,1)S(1)} custom-call(bf16[384,12288]{1,0:T(8,128)(2,1)} %adj.1, s32[64,64]{1,0:T(8,128)} %mask_h.1, bf16[200,384]{1,0:T(8,128)(2,1)} %bitcast.3, bf16[200,512]{1,0:T(8,128)(2,1)} %w1.1), custom_call_target="tpu_custom_call" | custom-call | tf_op jit(solution)/shard_map/gcn/pallas_call | solution.py:255
  63.7 0.0 copy-done
  63.7 1.0 %fusion = f32[384,107]{0,1:T(8,128)} fusion(bf16[384,512]{1,0:T(8,128)(2,1)S(1)} %gcn.1, bf16[512,107]{0,1:T(8,128)(2,1)S(1)} %copy-done), kind=kOutput, calls=%fused_computation | convolution fusion | flops 42074112 | bytes 667136 | tf_op jit(solution)/shard_map/dot_general | solution.py:284
Async XLA Ops:
  0.0 63.7 %copy-start = (bf16[512,107]{0,1:T(8,128)(2,1)S(1)}, bf16[512,107]{0,1:T(8,128)(2,1)}, u32[]{:S(2)}) copy-start(bf16[512,107]{0,1:T(8,128)(2,1)} %param.9) | copy-start | bytes 328708

commit v7 on v6

--- a/solution.py
+++ b/solution.py
@@ -11,8 +11,8 @@
 SLOTS = 96
 CHUNKS = 8, 4
 BAND = 32
-DIRECT = 9, 9, 4
-LEAD = 24
+DIRECT = (9, 9, 4), (9, 9, 4)
+LEAD = 3
 AXES = ('xyz', 'yzx', 'zxy')
 MESH = pl.DeviceIdType.MESH
 
@@ -22,12 +22,12 @@
     return sum(off[a] for a in before) % 2
 
 
-def piece_sends(is_src, p, zc, dy, dx):
+def piece_sends(layer, is_src, p, zc, dy, dx):
     off = {'x': dx, 'y': dy, 'z': zc}
     order = AXES[p]
     last, depth, direct = -1, 0, []
     for i, a in enumerate(order):
-        direct.append(depth >= DIRECT[i])
+        direct.append(depth >= DIRECT[layer][i])
         steps = (zc if is_src else 1 + zc) if a == 'z' else (0, 1, 2, 1)[off[a]]
         if steps:
             last = i
@@ -50,23 +50,24 @@
     return out
 
 
+ORDER_CODES = [
+    [32, 3136, 6224, 420, 353, 3500, 7747, 4292, 3216, 4684, 100, 6240, 6467, 6529, 3372, 7377, 1192, 195, 4994, 3900, 756, 8060, 1331, 7845,
+     1485, 8080, 532, 1602, 8903, 5765, 4357, 3777, 1639, 6387, 4781, 847, 3591, 6673, 6888, 1745, 1967, 3298, 4952, 1906, 1387, 7598, 5471, 591,
+     1069, 4532, 6920, 3964, 7878, 7455, 5897, 3069, 949, 2743, 5358, 4427, 8947, 5163, 2025, 2278, 8425, 6101, 2830, 6807, 9208, 8178, 8498, 3671,
+     5694, 4222, 1019, 2325, 5503, 7549, 2141, 7238, 8347, 2966, 4842, 5962, 2457, 4054, 8633, 2558, 8760, 9051, 5622, 2650, 5274, 7178, 8665, 7034],
+    [0, 3104, 6208, 368, 161, 3500, 7716, 452, 4291, 6241, 4656, 7331, 1228, 3249, 676, 6444, 4997, 225, 8147, 3363, 520, 1692, 7868, 1293,
+     1989, 3892, 1583, 6413, 4357, 6823, 1506, 783, 5839, 8848, 7981, 6626, 6545, 1908, 3624, 1415, 1779, 7921, 3278, 7666, 1067, 5415, 632, 7426,
+     8491, 4724, 3752, 4607, 8166, 949, 4924, 5151, 2249, 5949, 6967, 5367, 4489, 2766, 2025, 8371, 8981, 6118, 2872, 4149, 3022, 7511, 7275, 9158,
+     7037, 978, 6781, 2930, 3734, 3967, 2363, 5758, 2410, 8298, 5502, 4857, 5246, 6043, 9051, 2134, 7158, 2585, 2616, 4057, 8570, 8826, 8698, 5642],
+]
+
+
 def words(codes):
     return [(c // 32, c // 16 % 2, c // 4 % 4, c % 4) for c in codes]
 
 
-SRC_CODES = [
-    0, 32, 64, 3, 36, 80, 44, 4, 1, 48, 65, 67, 33, 35, 68, 76, 12, 2, 52, 40, 84, 7, 83, 81,
-    60, 13, 5, 15, 16, 17, 37, 45, 66, 92, 8, 39, 20, 49, 69, 18, 71, 19, 34, 79, 51, 14, 11, 56,
-    6, 77, 82, 47, 53, 61, 72, 28, 41, 85, 9, 55, 23, 21, 87, 63, 93, 43, 46, 29, 31, 95, 88, 38,
-    10, 70, 24, 59, 78, 73, 57, 30, 50, 22, 75, 86, 54, 62, 42, 26, 25, 89, 91, 74, 94, 58, 27, 90,
-]
-SINK_CODES = [
-    32, 64, 0, 80, 65, 44, 36, 3, 68, 67, 48, 76, 1, 4, 12, 35, 2, 81, 92, 40, 83, 60, 84, 69,
-    45, 16, 52, 66, 71, 5, 37, 33, 7, 15, 77, 79, 13, 72, 49, 82, 17, 39, 47, 56, 51, 43, 8, 34,
-    28, 14, 95, 6, 63, 93, 20, 41, 78, 55, 11, 19, 9, 87, 85, 53, 70, 21, 23, 73, 88, 18, 46, 38,
-    86, 75, 94, 31, 29, 10, 59, 50, 57, 61, 30, 91, 24, 42, 89, 22, 62, 90, 26, 54, 74, 25, 27, 58,
-]
-SRC_ORDER, SINK_ORDER = words(SRC_CODES), words(SINK_CODES)
+SRC_ORDER = [words([c // SLOTS for c in codes]) for codes in ORDER_CODES]
+SINK_ORDER = [words([c % SLOTS for c in codes]) for codes in ORDER_CODES]
 
 
 def kernel(adj, mask_h, h0t, w1, y_two, a_v, mask, w1_v, w1t, tab1, tab2, acc1, acc2, peer1, peer2,
@@ -93,40 +94,40 @@
     links = [(axis, d) for axis in 'xyz' for d in (1, -1, 2)]
     target = {link: rows_at(*link) for link in links}
 
+    loads = [pltpu.make_async_copy(src, dst, load_sem.at[i]) for i, (src, dst) in enumerate([(w1, w1_v), (mask_h, mask)])]
+    bands = [pl.ds(i * BAND, BAND) for i in range(BLOCK // BAND)]
+    adj_loads = [pltpu.make_async_copy(adj.at[rows], a_v.at[rows], adj_sem.at[i]) for i, rows in enumerate(bands)]
+
+    def slot_of(word):
+        p, zc, dy, dx = word
+        return grid[zc][dy][dx] + p
+
+    def send_piece(layer, tab, recv_sem, src_role, word):
+        slot = slot_of(word)
+        for link in piece_sends(layer, src_role, *word):
+            pltpu.make_async_remote_copy(
+                src_ref=tab.at[slot], dst_ref=tab.at[slot],
+                send_sem=send_sem.at[layer, 'xyz'.index(link[0])], recv_sem=recv_sem.at[slot],
+                device_id=(rep, target[link]), device_id_type=MESH).start()
+
+    def wait_piece(tab, recv_sem, word):
+        slot = slot_of(word)
+        pltpu.make_async_copy(tab.at[slot], tab.at[slot], recv_sem.at[slot]).wait()
+
+    own = [(p, 0, 0, 0) for p in range(3)]
+
+    own_loads = [pltpu.make_async_copy(h0t.at[:, pl.ds(p * PART, PART)], tab1.at[slot_of(own[p])], own_sem.at[p]) for p in range(3)]
+
+    @pl.when(is_src)
+    def _():
+        for copy in own_loads:
+            copy.start()
+
     barrier = pltpu.get_barrier_semaphore()
     for link in links:
         pl.semaphore_signal(barrier, inc=1, device_id=(rep, target[link]), device_id_type=MESH)
     pl.semaphore_signal(barrier, inc=1, device_id=(1 - rep, row), device_id_type=MESH)
 
-    loads = [pltpu.make_async_copy(src, dst, load_sem.at[i]) for i, (src, dst) in enumerate([(w1, w1_v), (mask_h, mask)])]
-    bands = [pl.ds(i * BAND, BAND) for i in range(BLOCK // BAND)]
-    adj_loads = [pltpu.make_async_copy(adj.at[rows], a_v.at[rows], adj_sem.at[i]) for i, rows in enumerate(bands)]
-
-    def slot_of(word):
-        p, zc, dy, dx = word
-        return grid[zc][dy][dx] + p
-
-    def send_piece(layer, tab, recv_sem, src_role, word):
-        slot = slot_of(word)
-        for link in piece_sends(src_role, *word):
-            pltpu.make_async_remote_copy(
-                src_ref=tab.at[slot], dst_ref=tab.at[slot],
-                send_sem=send_sem.at[layer, 'xyz'.index(link[0])], recv_sem=recv_sem.at[slot],
-                device_id=(rep, target[link]), device_id_type=MESH).start()
-
-    def wait_piece(tab, recv_sem, word):
-        slot = slot_of(word)
-        pltpu.make_async_copy(tab.at[slot], tab.at[slot], recv_sem.at[slot]).wait()
-
-    own = [(p, 0, 0, 0) for p in range(3)]
-
-    own_loads = [pltpu.make_async_copy(h0t.at[:, pl.ds(p * PART, PART)], tab1.at[slot_of(own[p])], own_sem.at[p]) for p in range(3)]
-
-    @pl.when(is_src)
-    def _():
-        for copy in own_loads:
-            copy.start()
-
     for copy in loads + adj_loads:
         copy.start()
 
@@ -147,10 +148,10 @@
     acc1[...] = jnp.zeros_like(acc1)
     acc2[...] = jnp.zeros_like(acc2)
 
-    def chunk_operands(tab, first, count):
+    def chunk_operands(layer, tab, first, count):
         a_parts, t_parts = [], []
         for n in range(first, first + count):
-            slot = lax.select(is_src, slot_of(SRC_ORDER[n]), slot_of(SINK_ORDER[n]))
+            slot = lax.select(is_src, slot_of(SRC_ORDER[layer][n]), slot_of(SINK_ORDER[layer][n]))
             keep = mask[row, rep * 32 + lax.div(slot, 3)].astype(jnp.float32).astype(jnp.bfloat16)
             a_parts.append(a_v[:, pl.ds(pl.multiple_of(slot * PART, PART), PART)])
             t_parts.append(tab[slot] * keep)
@@ -161,33 +162,36 @@
         @pl.when(is_src)
         def _():
             for n in words:
-                if SRC_ORDER[n] not in own:
-                    wait_piece(tab, recv_sem, SRC_ORDER[n])
-                    send_piece(layer, tab, recv_sem, True, SRC_ORDER[n])
+                if SRC_ORDER[layer][n] not in own:
+                    wait_piece(tab, recv_sem, SRC_ORDER[layer][n])
+                    send_piece(layer, tab, recv_sem, True, SRC_ORDER[layer][n])
 
         @pl.when(jnp.logical_not(is_src))
         def _():
             for n in words:
-                wait_piece(tab, recv_sem, SINK_ORDER[n])
-                send_piece(layer, tab, recv_sem, False, SINK_ORDER[n])
-
-    def gather(layer, tab, recv_sem, multiply, count, lead):
-        done = 0
-        for first in range(0, SLOTS, count):
+                wait_piece(tab, recv_sem, SINK_ORDER[layer][n])
+                send_piece(layer, tab, recv_sem, False, SINK_ORDER[layer][n])
+
+    def gather(layer, tab, recv_sem, multiply, size, lead):
+        bounds = [(first, size) for first in range(0, SLOTS - size, size)]
+        bounds += [(SLOTS - size, size // 2), (SLOTS - size // 2, size // 2)]
+        todo = []
+        for i, (first, count) in enumerate(bounds):
             relay(layer, tab, recv_sem, range(first, first + count))
-            if first + count < lead:
+            todo.append((first, count))
+            if i + 1 < lead:
                 continue
-            if layer == 0 and done == 0:
+            if layer == 0 and i + 1 == lead:
                 loads[1].wait()
                 for copy in adj_loads:
                     copy.wait()
-            for _ in range(2):
-                if done <= first:
-                    multiply(*chunk_operands(tab, done, count))
-                    done += count
+            for chunk in todo[:2]:
+                multiply(*chunk_operands(layer, tab, *chunk))
+            todo = todo[2:]
+        assert not todo
 
     def multiply1(a, t):
-        acc1[...] += lax.dot_general(a, t, (((1,), (1,)), ((), ())), preferred_element_type=jnp.float32)
+        acc1[:, :F0] += lax.dot_general(a, t, (((1,), (1,)), ((), ())), preferred_element_type=jnp.float32)
 
     def multiply2(a, t):
         zt = jnp.dot(w1t[...], t, preferred_element_type=jnp.float32)
@@ -214,12 +218,12 @@
     def _():
         for p in range(3):
             swap1[p].wait_recv()
-            part = acc1[parts[p], :] + peer1[parts[p], :]
+            part = acc1[parts[p], :F0] + peer1[parts[p], :F0]
             tab2[slot_of(own[p])] = part.T.astype(jnp.bfloat16)
         for p in range(3):
             send_piece(1, tab2, recv_sem2, True, own[p])
 
-    gather(1, tab2, recv_sem2, multiply2, CHUNKS[1], 0)
+    gather(1, tab2, recv_sem2, multiply2, CHUNKS[1], 1)
     swap2 = to_peer(1, acc2, peer2)
     for copy in swap2:
         copy.start()
@@ -230,8 +234,8 @@
     def drain(role):
         for layer, tab in ((0, tab1), (1, tab2)):
             for i, axis in enumerate('xyz'):
-                words = SRC_ORDER if role else SINK_ORDER
-                count = sum(link[0] == axis for word in words for link in piece_sends(role, *word))
+                words = SRC_ORDER[layer] if role else SINK_ORDER[layer]
+                count = sum(link[0] == axis for word in words for link in piece_sends(layer, role, *word))
                 ref = tab.at[pl.ds(0, count)]
                 pltpu.make_async_copy(ref, ref, send_sem.at[layer, i]).wait()
 
@@ -265,9 +269,9 @@
                 pltpu.VMEM((F1, F0), jnp.bfloat16),
                 pltpu.VMEM((SLOTS, F0, PART), jnp.bfloat16),
                 pltpu.VMEM((SLOTS, F0, PART), jnp.bfloat16),
-                pltpu.VMEM((BLOCK, F0), jnp.float32),
+                pltpu.VMEM((BLOCK, 256), jnp.float32),
                 pltpu.VMEM((BLOCK, F1), jnp.float32),
-                pltpu.VMEM((BLOCK, F0), jnp.float32),
+                pltpu.VMEM((BLOCK, 256), jnp.float32),
                 pltpu.VMEM((BLOCK, F1), jnp.float32),
                 pltpu.SemaphoreType.DMA((2,)),
                 pltpu.SemaphoreType.DMA((BLOCK // BAND,)),

time: 64.8 us -> 63.2 us (0.975)
  Pallas kernels: 63.7 us -> 62.2 us
    pallas_call x1, Pallas kernels: 63.7 us -> 62.2 us  [step(): pl.pallas_call(kernel, name='gcn', out_shape=jax.ShapeDtypeStruct((BLOCK,...]
where the time goes in v7:
time: 63.2 us; the launch traced here: 63.1 us
  Pallas kernels  62.2 us (98%)
  matrix products  0.96 us (2%)
    pallas_call x1, Pallas kernels, step(): pl.pallas_call(kernel, name='gcn', out_shape=jax.ShapeDtypeStruct((BLOCK,...  62.2 us

profile of v7, /device:TPU:1, one launch (start us, length us, event | category | flops | bytes accessed | tf_op | source)
XLA Modules:
  0.0 63.1 jit_solution(10239311727486634962)
XLA Ops:
  0.0 0.0 copy-start
  0.0 62.2 %gcn.1 = bf16[384,512]{1,0:T(8,128)(2,1)S(1)} custom-call(bf16[384,12288]{1,0:T(8,128)(2,1)} %adj.1, s32[64,64]{1,0:T(8,128)} %mask_h.1, bf16[200,384]{1,0:T(8,128)(2,1)} %bitcast.3, bf16[200,512]{1,0:T(8,128)(2,1)} %w1.1), custom_call_target="tpu_custom_call" | custom-call | tf_op jit(solution)/shard_map/gcn/pallas_call | solution.py:259
  62.2 0.0 copy-done
  62.2 1.0 %fusion = f32[384,107]{0,1:T(8,128)} fusion(bf16[384,512]{1,0:T(8,128)(2,1)S(1)} %gcn.1, bf16[512,107]{0,1:T(8,128)(2,1)S(1)} %copy-done), kind=kOutput, calls=%fused_computation | convolution fusion | flops 42074112 | bytes 667136 | tf_op jit(solution)/shard_map/dot_general | solution.py:288
Async XLA Ops:
  0.0 62.2 %copy-start = (bf16[512,107]{0,1:T(8,128)(2,1)S(1)}, bf16[512,107]{0,1:T(8,128)(2,1)}, u32[]{:S(2)}) copy-start(bf16[512,107]{0,1:T(8,128)(2,1)} %param.9) | copy-start | bytes 328708

commit v8 on v7

--- a/solution.py
+++ b/solution.py
@@ -220,8 +220,9 @@
             swap1[p].wait_recv()
             part = acc1[parts[p], :F0] + peer1[parts[p], :F0]
             tab2[slot_of(own[p])] = part.T.astype(jnp.bfloat16)
-        for p in range(3):
-            send_piece(1, tab2, recv_sem2, True, own[p])
+            if p:
+                send_piece(1, tab2, recv_sem2, True, own[p - 1])
+        send_piece(1, tab2, recv_sem2, True, own[2])
 
     gather(1, tab2, recv_sem2, multiply2, CHUNKS[1], 1)
     swap2 = to_peer(1, acc2, peer2)

time: 63.2 us -> 63.1 us (level)
  no operation moved by 1% of the time
where the time goes in v8:
time: 63.1 us; the launch traced here: 63 us
  Pallas kernels  62.1 us (98%)
  matrix products  0.96 us (2%)
    pallas_call x1, Pallas kernels, step(): pl.pallas_call(kernel, name='gcn', out_shape=jax.ShapeDtypeStruct((BLOCK,...  62.1 us

profile of v8, /device:TPU:1, one launch (start us, length us, event | category | flops | bytes accessed | tf_op | source)
XLA Modules:
  0.0 63.0 jit_solution(5786136281742130578)
XLA Ops:
  0.0 0.0 copy-start
  0.0 62.1 %gcn.1 = bf16[384,512]{1,0:T(8,128)(2,1)S(1)} custom-call(bf16[384,12288]{1,0:T(8,128)(2,1)} %adj.1, s32[64,64]{1,0:T(8,128)} %mask_h.1, bf16[200,384]{1,0:T(8,128)(2,1)} %bitcast.3, bf16[200,512]{1,0:T(8,128)(2,1)} %w1.1), custom_call_target="tpu_custom_call" | custom-call | tf_op jit(solution)/shard_map/gcn/pallas_call | solution.py:260
  62.1 0.0 copy-done
  62.1 1.0 %fusion = f32[384,107]{0,1:T(8,128)} fusion(bf16[384,512]{1,0:T(8,128)(2,1)S(1)} %gcn.1, bf16[512,107]{0,1:T(8,128)(2,1)S(1)} %copy-done), kind=kOutput, calls=%fused_computation | convolution fusion | flops 42074112 | bytes 667136 | tf_op jit(solution)/shard_map/dot_general | solution.py:289
Async XLA Ops:
  0.0 62.1 %copy-start = (bf16[512,107]{0,1:T(8,128)(2,1)S(1)}, bf16[512,107]{0,1:T(8,128)(2,1)}, u32[]{:S(2)}) copy-start(bf16[512,107]{0,1:T(8,128)(2,1)} %param.9) | copy-start | bytes 328708
